TPU v7x, 256 devices: a whole 4x4x8 slice. The times are simulated.
256 devices in a mesh: gx: 16 (over z, x_hi), gy: 8 (over y, core), col: 2 (over x_lo).
Axes of the slice: x: 4 (x_hi: 2, x_lo: 2; x = x_hi * 2 + x_lo), y: 4, z: 8, core: 2. Of those that a mesh axis runs over, the one named last changes fastest.
Arguments:
- sources: float32 [16, 8, 2, 128, 1152], P('gx', 'gy', None, 'col'), may hold values from -100 to 100
- impedance: bfloat16 [16, 8, 2, 1152, 1152], P('gx', 'gy'), may hold values from -0.09375 to 0.09375
- pair_maps: bfloat16 [16, 8, 2, 2, 384, 384], P('gx', 'gy'), may hold values from -0.21875 to 0.21875
- lead_side: int32 [16, 8, 2], P('gx', 'gy'), may hold values from 0 to 1
- coarse_basis: float32 [16, 8, 32, 2, 1152], P('gx', 'gy'), may hold values from -0.125 to 0.125
- coarse_inverse: float32 [4096, 4096], P(('gx', 'gy', 'col')), may hold values from -0.6 to 0.6
Outputs:
- solution_traces: float32 [16, 8, 2, 128, 1152], P('gx', 'gy', None, 'col')
Inputs may be any that keep to these rules, and one draw needn't show every extreme that they name: `lead_side`: entries of interfaces beyond the last subdomain along a dimension are read by no step.
All inputs are finite; a program needn't handle non-finite values.
Results may differ from a plain program's by a relative error of at most 0.0039.
Values may be sent and summed in bfloat16 or wider, within the bound.
A program may use at most 64 MiB of HBM per device.

v0:
```python
import jax
import jax.numpy as jnp
from jax import lax
from jax.sharding import Mesh
from jax.sharding import PartitionSpec as P

ITERS = 2
GX = ("gx_0", "gx_1")
GY = ("gy_0", "gy_1")
GX_GY_COL = ("gx_0", "gx_1", "gy_0", "gy_1", "col")


STEP_RATIO = 0.4


def copy_for_each(array, axis):
    copies = jnp.broadcast_to(array, (lax.axis_size(axis), *array.shape))
    return lax.all_to_all(copies, axis, split_axis=0, concat_axis=0, tiled=True)


def in_order(pieces, dim):
    pieces = jnp.moveaxis(pieces, 0, dim)
    shape = pieces.shape
    return pieces.reshape(*shape[:dim], shape[dim] * shape[dim + 1], *shape[dim + 2 :])


def gather_directly(array, axis, dim):
    pieces = copy_for_each(array, axis)
    return in_order(pieces, dim)


def shifted(block, axis, distance):
    devices = range(lax.axis_size(axis))
    route = [(i - distance, i) for i in devices if i - distance in devices]
    return lax.ppermute(block, axis, route)


def whole_of(array, axes, dim):
    far, near = axes
    pieces = copy_for_each(copy_for_each(array, far), near)
    return in_order(pieces.swapaxes(0, 1).reshape(-1, *array.shape), dim)


def taken_together(array, axis):
    return copy_for_each(array, axis).sum(axis=0)


def by_axis(array, axes):
    far, near = axes
    return taken_together(taken_together(array, near), far)


def packed_total(arrays, axis):
    ends = [0]
    for a in arrays:
        ends.append(ends[-1] + a.size)
    subtotal = by_axis(jnp.concatenate([a.ravel() for a in arrays]), axis)
    return tuple((subtotal[b:e].reshape(a.shape) for a, b, e in zip(arrays, ends, ends[1:])))


def complex_apply(traces, real_part, imag_part):
    sources_here = traces.shape[1]
    flattened = traces.reshape(2 * sources_here, traces.shape[2])
    first_part = jnp.dot(flattened, real_part, preferred_element_type=jnp.float32).reshape(
        2, sources_here, -1
    )
    second_part = jnp.dot(flattened, imag_part, preferred_element_type=jnp.float32).reshape(
        2, sources_here, -1
    )
    return jnp.stack([first_part[0] - second_part[1], second_part[0] + first_part[1]])


def pair_solve(lower_side, upper_side, solver):
    return complex_apply(jnp.concatenate([lower_side, upper_side], axis=2), solver[0], solver[1])


def orient(solver, leading, face_width):
    swapped = jnp.roll(solver, (face_width, face_width), axis=(1, 2))
    return jnp.where(leading == 0, solver, swapped)


def per_device(sources, impedance, pair_maps, lead_side, coarse_basis, coarse_inverse):
    drive_traces = sources[0, 0]
    sources_here = drive_traces.shape[1]
    face_width = drive_traces.shape[2] // 6
    map_real = impedance[0, 0, 0]
    map_imag = impedance[0, 0, 1]
    basis_here = coarse_basis[0, 0]
    coarse_count = basis_here.shape[0]
    first_count = lax.axis_size(GX)
    second_count = lax.axis_size(GY)
    first_index = lax.axis_index(GX)
    second_index = lax.axis_index(GY)
    first_solver = orient(pair_maps[0, 0, 0], lead_side[0, 0, 0], face_width)
    second_solver = orient(pair_maps[0, 0, 1], lead_side[0, 0, 1], face_width)
    pair_rows = gather_directly(coarse_inverse, "col", 0)
    row_blocks = pair_rows.reshape(coarse_count, -1, coarse_count)
    iterate = jnp.zeros(drive_traces.shape, jnp.float32)
    for repeat in range(ITERS):
        rounded = iterate.astype(jnp.bfloat16)
        outgoing = (complex_apply(rounded, map_real, map_imag) + drive_traces).astype(jnp.bfloat16)
        first_faces = outgoing[:, :, : 2 * face_width].reshape(2, sources_here, 2, face_width)
        second_faces = outgoing[:, :, 2 * face_width : 4 * face_width].reshape(
            2, sources_here, 2, face_width
        )
        first_above = shifted(first_faces[:, :, 0], GX, -1)
        second_above = shifted(second_faces[:, :, 0], GY, -1)
        first_solved = pair_solve(first_faces[:, :, 1], first_above, first_solver)
        second_solved = pair_solve(second_faces[:, :, 1], second_above, second_solver)
        face_one = first_solved[:, :, :face_width]
        face_three = second_solved[:, :, :face_width]
        face_zero = shifted(first_solved[:, :, face_width:], GX, 1)
        face_two = shifted(second_solved[:, :, face_width:], GY, 1)
        face_one = jnp.where(first_index < first_count - 1, face_one, 0.0)
        face_three = jnp.where(second_index < second_count - 1, face_three, 0.0)
        updated = jnp.concatenate(
            [
                face_zero,
                face_one,
                face_two,
                face_three,
                outgoing[:, :, 5 * face_width :].astype(jnp.float32),
                outgoing[:, :, 4 * face_width : 5 * face_width].astype(jnp.float32),
            ],
            axis=2,
        )
        defect = updated - iterate
        projected = jnp.einsum("csk,pck->sp", defect, basis_here, precision=lax.Precision.HIGHEST)
        gathered = whole_of(projected[None], (("gx_0", "gx_1", "gy_0"), "gy_1"), 0)
        coarse = jnp.einsum("nsp,qnp->sq", gathered, row_blocks, precision=lax.Precision.HIGHEST)
        correction = jnp.einsum("sp,pck->csk", coarse, basis_here, precision=lax.Precision.HIGHEST)
        defect_norm, correction_norm = packed_total(
            (jnp.sum(defect * defect, axis=(0, 2)), jnp.sum(correction * correction, axis=(0, 2))),
            (("gx_0", "gx_1"), ("gy_0", "gy_1")),
        )
        factor = STEP_RATIO * jnp.sqrt(defect_norm / (correction_norm + 1e-06))
        iterate = updated + factor[None, :, None] * correction
    return iterate[None, None]


def solution(mesh):
    finer = Mesh(
        mesh.devices.reshape(8, 2, 4, 2, mesh.shape["col"]), ("gx_0", "gx_1", "gy_0", "gy_1", "col")
    )
    return jax.shard_map(
        per_device,
        mesh=finer,
        in_specs=(
            P(GX, GY, None, "col", None),
            P(GX, GY, None, None, None),
            P(GX, GY, None, None, None, None),
            P(GX, GY, None),
            P(GX, GY, None, None, None),
            P(GX_GY_COL, None),
        ),
        out_specs=P(GX, GY, None, "col", None),
        check_vma=False,
    )
```

profile of v0, /device:TPU:1, one launch (start us, length us, event | category | flops | bytes accessed | tf_op | source)
XLA Modules:
  0.0 224.3 jit_solution(4108779847346650157)
XLA Ops:
  0.0 2.4 %fusion.2 = f32[128,1152]{1,0:T(8,128)S(1)} fusion(bf16[1,1,2,1152,1152]{4,3,2,1,0:T(8,128)(2,1)} %param.7), kind=kOutput, calls=%fused_computation.2 | convolution fusion | flops 339738624 | bytes 3244032 | tf_op jit(solution)/shard_map/dot_general | solution.py:67
  2.4 2.4 %fusion.6 = f32[128,1152]{1,0:T(8,128)S(1)} fusion(bf16[1,1,2,1152,1152]{4,3,2,1,0:T(8,128)(2,1)} %param.7), kind=kOutput, calls=%fused_computation.6 | convolution fusion | flops 339738624 | bytes 3244032 | tf_op jit(solution)/shard_map/dot_general | solution.py:64
  6.6 5.1 %collective-permute-start.2 = (bf16[2,64,192]{2,1,0:T(8,128)(2,1)}, bf16[2,64,192]{2,1,0:T(8,128)(2,1)}, u32[]{:S(2)}, u32[]{:S(2)}) collective-permute-start(bf16[2,64,192]{2,1,0:T(8,128)(2,1)} %bitcast.135), channel_id=1, source_target_pairs={{2,0},{4,2},{6,4},{8,6},{10,8},{12,10},{14,12},{3,1},{5,3},{7,5},{... | collective-permute-start | bytes 147464 | tf_op jit(solution)/shard_map/ppermute | solution.py:35
  13.3 1.4 collective-permute-start
  15.6 3.5 %all-to-all-start.2 = ((f32[2,16,4096]{2,1,0:T(8,128)}), f32[2,16,4096]{2,1,0:T(8,128)S(1)}, u32[]{:S(2)}, u32[]{:S(2)}) async-start(f32[2,16,4096]{2,1,0:T(8,128)} %broadcast_in_dim.45), calls=%async_computation.2 | async-start | bytes 1048576 | tf_op jit(solution)/shard_map/all_to_all | solution.py:18
  22.5 1.0 copy.83
  23.5 1.1 fusion.36
  24.6 1.1 fusion.34
  25.8 1.1 fusion.32
  26.9 1.1 fusion.30
  28.1 1.9 collective-permute-start.3
  30.2 5.5 %collective-permute-start.1 = (f32[2,64,192]{2,1,0:T(8,128)S(1)}, f32[2,64,192]{2,1,0:T(8,128)S(1)}, u32[]{:S(2)}, u32[]{:S(2)}) collective-permute-start(f32[2,64,192]{2,1,0:T(8,128)S(1)} %get-tuple-element.42), channel_id=1, source_target_pairs={{0,16},{16,32},{32,48},{48,64},{64,80},{80,96},{96,112},{112,128},... | collective-permute-start | bytes 294920 | tf_op jit(solution)/shard_map/ppermute | solution.py:35
  35.8 2.2 collective-permute-done.1
  38.0 1.1 concatenate.68
  39.9 1.5 reshape.170
  41.4 17.1 %all-to-all-start = ((f32[64,1,2048]{2,1,0:T(1,128)}), f32[64,1,2048]{2,1,0:T(1,128)}, u32[]{:S(2)}, u32[]{:S(2)}) async-start(f32[64,1,2048]{2,1,0:T(1,128)} %reshape.170), calls=%async_computation | async-start | bytes 1048576 | tf_op jit(solution)/shard_map/all_to_all | solution.py:18
  60.1 14.8 %all-to-all-done = f32[64,1,2048]{2,1,0:T(1,128)} async-done(((f32[64,1,2048]{2,1,0:T(1,128)}), f32[64,1,2048]{2,1,0:T(1,128)}, u32[]{:S(2)}, u32[]{:S(2)}) %all-to-all-start) | async-done | bytes 524320 | tf_op jit(solution)/shard_map/all_to_all | solution.py:18
  75.5 3.0 %reduce.6 = f32[64,2048]{1,0:T(8,128)S(1)} reduce(f32[64,1,2048]{2,1,0:T(1,128)} %all-to-all-done, f32[]{:T(128)} %broadcast.35), dimensions={1}, to_apply=%all_to_all.35.reduce_sub_computation | reduce | bytes 1048580 | tf_op jit(solution)/shard_map/all_to_all | solution.py:18
  79.3 2.1 reshape.172
  81.4 8.4 %all_to_all.55 = f32[2,1,131072]{2,1,0:T(1,128)S(1)} all-to-all(f32[2,1,131072]{2,1,0:T(1,128)} %reshape.172), channel_id=1, replica_groups=mesh['gx_0'=8,'gx_1'=2,'gy_0'=4,'gy_1'=2,'col'=2] {'gy_1'}, dimensions={0} | all-to-all | bytes 2097152 | tf_op jit(solution)/shard_map/all_to_all | solution.py:18
  89.8 5.0 %reduce.7 = f32[2,131072]{1,0:T(2,128)} reduce(f32[2,1,131072]{2,1,0:T(1,128)S(1)} %all_to_all.55, f32[]{:T(128)} %broadcast.35), dimensions={1}, to_apply=%all_to_all.37.reduce_sub_computation | reduce | bytes 2097156 | tf_op jit(solution)/shard_map/all_to_all | solution.py:18
  94.8 2.4 %reshape.173 = f32[2,1,64,32,64]{4,3,2,1,0:T(8,128)S(1)} reshape(f32[2,131072]{1,0:T(2,128)} %reduce.7) | data formatting | bytes 2097152
  97.6 2.5 %fusion.14 = f32[64,32,1]{0,1,2:T(8,128)S(1)} fusion(f32[32,128,32]{1,0,2:T(8,128)S(1)} %copy.68, f32[128,64,32]{1,2,0:T(8,128)S(1)} %bitcast.142), kind=kOutput, calls=%fused_computation.14 | convolution fusion | flops 100663296 | bytes 1581056 | tf_op jit(solution)/shard_map/nsp,qnp->sq/dot_general | solution.py:130
  101.0 8.8 %all_to_all.56 = f32[8,1,128]{2,1,0:T(1,128)S(1)} all-to-all(f32[8,1,128]{2,1,0:T(1,128)S(1)} %broadcast_in_dim.46), channel_id=1, replica_groups=mesh['gx_0'=8,'gx_1'=2,'gy_0'=4,'gy_1'=2,'col'=2] {'gy_0','gy_1'}, dimensions={0} | all-to-all | bytes 8192 | tf_op jit(solution)/shard_map/all_to_all | solution.py:18
  109.8 11.7 %all_to_all.57 = f32[16,1,128]{2,1,0:T(1,128)S(1)} all-to-all(f32[16,1,128]{2,1,0:T(1,128)S(1)} %broadcast_in_dim.47), channel_id=1, replica_groups=mesh['gx_0'=8,'gx_1'=2,'gy_0'=4,'gy_1'=2,'col'=2] {'gx_0','gx_1'}, dimensions={0} | all-to-all | bytes 16384 | tf_op jit(solution)/shard_map/all_to_all | solution.py:18
  121.8 2.3 %fusion = f32[128,1152]{1,0:T(8,128)S(1)} fusion(bf16[128,1152]{1,0:T(8,128)(2,1)S(1)} %bitcast.151, bf16[1,1,2,1152,1152]{4,3,2,1,0:T(8,128)(2,1)} %param.7), kind=kOutput, calls=%fused_computation | convolution fusion | flops 339738624 | bytes 3538944 | tf_op jit(solution)/shard_map/dot_general | solution.py:67
  124.1 2.4 %fusion.4 = f32[128,1152]{1,0:T(8,128)S(1)} fusion(bf16[128,1152]{1,0:T(8,128)(2,1)S(1)} %bitcast.152, bf16[1,1,2,1152,1152]{4,3,2,1,0:T(8,128)(2,1)} %param.7), kind=kOutput, calls=%fused_computation.4 | convolution fusion | flops 339738624 | bytes 3538944 | tf_op jit(solution)/shard_map/dot_general | solution.py:64
  127.7 4.0 %collective-permute-start.6 = (bf16[2,64,192]{2,1,0:T(8,128)(2,1)}, bf16[2,64,192]{2,1,0:T(8,128)(2,1)}, u32[]{:S(2)}, u32[]{:S(2)}) collective-permute-start(bf16[2,64,192]{2,1,0:T(8,128)(2,1)} %bitcast.133), channel_id=1, source_target_pairs={{2,0},{4,2},{6,4},{8,6},{10,8},{12,10},{14,12},{3,1},{5,3},{7,5},{... | collective-permute-start | bytes 147464 | tf_op jit(solution)/shard_map/ppermute | solution.py:35
  132.1 1.3 collective-permute-start.4
  134.1 1.1 fusion.35
  135.2 1.1 fusion.33
  136.4 2.9 %collective-permute-done.4 = bf16[2,64,192]{2,1,0:T(8,128)(2,1)S(1)} collective-permute-done((bf16[2,64,192]{2,1,0:T(8,128)(2,1)S(1)}, bf16[2,64,192]{2,1,0:T(8,128)(2,1)S(1)}, u32[]{:S(2)}, u32[]{:S(2)}) %collective-permute-start.4) | collective-permute-done | bytes 49184 | tf_op jit(solution)/shard_map/ppermute | solution.py:35
  139.9 2.8 %collective-permute-start.7 = (f32[2,64,192]{2,1,0:T(8,128)S(1)}, f32[2,64,192]{2,1,0:T(8,128)S(1)}, u32[]{:S(2)}, u32[]{:S(2)}) collective-permute-start(f32[2,64,192]{2,1,0:T(8,128)S(1)} %get-tuple-element.36), channel_id=1, source_target_pairs={{0,2},{2,4},{4,6},{6,8},{8,10},{10,12},{12,14},{1,3},{3,5},{5,7},{... | collective-permute-start | bytes 294920 | tf_op jit(solution)/shard_map/ppermute | solution.py:35
  142.9 3.3 %collective-permute-start.5 = (f32[2,64,192]{2,1,0:T(8,128)S(1)}, f32[2,64,192]{2,1,0:T(8,128)S(1)}, u32[]{:S(2)}, u32[]{:S(2)}) collective-permute-start(f32[2,64,192]{2,1,0:T(8,128)S(1)} %get-tuple-element.38), channel_id=1, source_target_pairs={{0,16},{16,32},{32,48},{48,64},{64,80},{80,96},{96,112},{112,128},... | collective-permute-start | bytes 294920 | tf_op jit(solution)/shard_map/ppermute | solution.py:35
  146.3 2.9 %collective-permute-done.5 = f32[2,64,192]{2,1,0:T(8,128)S(1)} collective-permute-done((f32[2,64,192]{2,1,0:T(8,128)S(1)}, f32[2,64,192]{2,1,0:T(8,128)S(1)}, u32[]{:S(2)}, u32[]{:S(2)}) %collective-permute-start.5) | collective-permute-done | bytes 98336 | tf_op jit(solution)/shard_map/ppermute | solution.py:35
  150.0 1.1 broadcast_bitcast_fusion.2
  151.1 2.7 %reshape.174 = f32[64,1,2048]{2,1,0:T(1,128)} reshape(f32[64,1,32,64]{3,2,1,0:T(8,128)} %broadcast_bitcast_fusion.2) | data formatting | bytes 1048576
  153.8 7.9 %all-to-all-start.5 = ((f32[64,1,2048]{2,1,0:T(1,128)}), f32[64,1,2048]{2,1,0:T(1,128)S(1)}, u32[]{:S(2)}, u32[]{:S(2)}) async-start(f32[64,1,2048]{2,1,0:T(1,128)} %reshape.174), calls=%async_computation.5 | async-start | bytes 1048576 | tf_op jit(solution)/shard_map/all_to_all | solution.py:18
  161.9 17.1 %all-to-all-done.5 = f32[64,1,2048]{2,1,0:T(1,128)S(1)} async-done(((f32[64,1,2048]{2,1,0:T(1,128)}), f32[64,1,2048]{2,1,0:T(1,128)S(1)}, u32[]{:S(2)}, u32[]{:S(2)}) %all-to-all-start.5) | async-done | bytes 524320 | tf_op jit(solution)/shard_map/all_to_all | solution.py:18
  179.0 1.9 reduce.8
  181.8 2.1 reshape.176
  183.9 7.6 %all_to_all.58 = f32[2,1,131072]{2,1,0:T(1,128)S(1)} all-to-all(f32[2,1,131072]{2,1,0:T(1,128)} %reshape.176), channel_id=1, replica_groups=mesh['gx_0'=8,'gx_1'=2,'gy_0'=4,'gy_1'=2,'col'=2] {'gy_1'}, dimensions={0} | all-to-all | bytes 2097152 | tf_op jit(solution)/shard_map/all_to_all | solution.py:18
  191.5 5.0 %reduce.9 = f32[2,131072]{1,0:T(2,128)} reduce(f32[2,1,131072]{2,1,0:T(1,128)S(1)} %all_to_all.58, f32[]{:T(128)} %broadcast.35), dimensions={1}, to_apply=%all_to_all.43.reduce_sub_computation | reduce | bytes 2097156 | tf_op jit(solution)/shard_map/all_to_all | solution.py:18
  196.5 2.4 %reshape.177 = f32[2,1,64,32,64]{4,3,2,1,0:T(8,128)S(1)} reshape(f32[2,131072]{1,0:T(2,128)} %reduce.9) | data formatting | bytes 2097152
  199.3 2.5 %fusion.12 = f32[64,32,1]{0,1,2:T(8,128)S(1)} fusion(f32[32,128,32]{1,0,2:T(8,128)S(1)} %copy.68, f32[128,64,32]{1,2,0:T(8,128)S(1)} %bitcast.141), kind=kOutput, calls=%fused_computation.12 | convolution fusion | flops 100663296 | bytes 1581056 | tf_op jit(solution)/shard_map/nsp,qnp->sq/dot_general | solution.py:130
  202.6 8.7 %all_to_all.59 = f32[8,1,128]{2,1,0:T(1,128)S(1)} all-to-all(f32[8,1,128]{2,1,0:T(1,128)S(1)} %broadcast_in_dim.50), channel_id=1, replica_groups=mesh['gx_0'=8,'gx_1'=2,'gy_0'=4,'gy_1'=2,'col'=2] {'gy_0','gy_1'}, dimensions={0} | all-to-all | bytes 8192 | tf_op jit(solution)/shard_map/all_to_all | solution.py:18
  211.4 11.8 %all_to_all.60 = f32[16,1,128]{2,1,0:T(1,128)S(1)} all-to-all(f32[16,1,128]{2,1,0:T(1,128)S(1)} %broadcast_in_dim.51), channel_id=1, replica_groups=mesh['gx_0'=8,'gx_1'=2,'gy_0'=4,'gy_1'=2,'col'=2] {'gx_0','gx_1'}, dimensions={0} | all-to-all | bytes 16384 | tf_op jit(solution)/shard_map/all_to_all | solution.py:18
  223.3 0.9 fusion.22
  (104 shorter events, 18.0 us)
Async XLA Ops:
  0.0 39.2 %copy-start = (f32[1,1,32,2,1152]{4,3,2,1,0:T(2,128)S(1)}, f32[1,1,32,2,1152]{4,3,2,1,0:T(2,128)}, u32[]{:S(2)}) copy-start(f32[1,1,32,2,1152]{4,3,2,1,0:T(2,128)} %param.10) | copy-start | bytes 884740
  2.4 2.5 %copy-start.6 = (f32[1,1,2,64,1152]{4,3,2,1,0:T(8,128)S(1)}, f32[1,1,2,64,1152]{4,3,2,1,0:T(8,128)}, u32[]{:S(2)}) copy-start(f32[1,1,2,64,1152]{4,3,2,1,0:T(8,128)} %param.6) | copy-start | bytes 1769476
  4.9 9.9 %copy-start.9 = (f32[16,4096]{1,0:T(8,128)S(1)}, f32[16,4096]{1,0:T(8,128)}, u32[]{:S(2)}) copy-start(f32[16,4096]{1,0:T(8,128)} %param.11) | copy-start | bytes 786436
  5.0 14.1 %copy-start.5 = (bf16[1,1,2,2,384,384]{5,4,3,2,1,0:T(8,128)(2,1)S(1)}, bf16[1,1,2,2,384,384]{5,4,3,2,1,0:T(8,128)(2,1)}, u32[]{:S(2)}) copy-start(bf16[1,1,2,2,384,384]{5,4,3,2,1,0:T(8,128)(2,1)} %param.8) | copy-start | bytes 3538948
  6.6 16.9 %collective-permute-start.2 = (bf16[2,64,192]{2,1,0:T(8,128)(2,1)}, bf16[2,64,192]{2,1,0:T(8,128)(2,1)}, u32[]{:S(2)}, u32[]{:S(2)}) collective-permute-start(bf16[2,64,192]{2,1,0:T(8,128)(2,1)} %bitcast.135), channel_id=1, source_target_pairs={{2,0},{4,2},{6,4},{8,6},{10,8},{12,10},{14,12},{3,1},{5,3},{7,5},{... | collective-permute-start | bytes 147464 | tf_op jit(solution)/shard_map/ppermute | solution.py:35
  13.3 5.9 %copy-start.11 = (s32[1,1,2]{2,1,0:T(1,128)S(1)}, s32[1,1,2]{2,1,0:T(1,128)}, u32[]{:S(2)}) copy-start(s32[1,1,2]{2,1,0:T(1,128)} %param.9) | copy-start | bytes 28
  13.3 12.4 %collective-permute-start = (bf16[2,64,192]{2,1,0:T(8,128)(2,1)}, bf16[2,64,192]{2,1,0:T(8,128)(2,1)}, u32[]{:S(2)}, u32[]{:S(2)}) collective-permute-start(bf16[2,64,192]{2,1,0:T(8,128)(2,1)} %bitcast.136), channel_id=1, source_target_pairs={{16,0},{32,16},{48,32},{64,48},{80,64},{96,80},{112,96},{128,112},... | collective-permute-start | bytes 147464 | tf_op jit(solution)/shard_map/ppermute | solution.py:35
  15.6 25.8 %all-to-all-start.2 = ((f32[2,16,4096]{2,1,0:T(8,128)}), f32[2,16,4096]{2,1,0:T(8,128)S(1)}, u32[]{:S(2)}, u32[]{:S(2)}) async-start(f32[2,16,4096]{2,1,0:T(8,128)} %broadcast_in_dim.45), calls=%async_computation.2 | async-start | bytes 1048576 | tf_op jit(solution)/shard_map/all_to_all | solution.py:18
  21.6 0.9 copy-start.8
  22.2 7.9 %copy-start.1 = (bf16[2,384,384]{2,1,0:T(8,128)(2,1)}, bf16[2,384,384]{2,1,0:T(8,128)(2,1)S(1)}, u32[]{:S(2)}) copy-start(bf16[2,384,384]{2,1,0:T(8,128)(2,1)S(1)} %get-tuple-element.10) | copy-start | bytes 1769476
  22.2 7.9 %copy-start.3 = (bf16[2,384,384]{2,1,0:T(8,128)(2,1)}, bf16[2,384,384]{2,1,0:T(8,128)(2,1)S(1)}, u32[]{:S(2)}) copy-start(bf16[2,384,384]{2,1,0:T(8,128)(2,1)S(1)} %get-tuple-element.9) | copy-start | bytes 1769476
  28.1 7.7 %collective-permute-start.3 = (f32[2,64,192]{2,1,0:T(8,128)S(1)}, f32[2,64,192]{2,1,0:T(8,128)S(1)}, u32[]{:S(2)}, u32[]{:S(2)}) collective-permute-start(f32[2,64,192]{2,1,0:T(8,128)S(1)} %get-tuple-element.40), channel_id=1, source_target_pairs={{0,2},{2,4},{4,6},{6,8},{8,10},{10,12},{12,14},{1,3},{3,5},{5,7},{... | collective-permute-start | bytes 294920 | tf_op jit(solution)/shard_map/ppermute | solution.py:35
  30.2 7.8 %collective-permute-start.1 = (f32[2,64,192]{2,1,0:T(8,128)S(1)}, f32[2,64,192]{2,1,0:T(8,128)S(1)}, u32[]{:S(2)}, u32[]{:S(2)}) collective-permute-start(f32[2,64,192]{2,1,0:T(8,128)S(1)} %get-tuple-element.42), channel_id=1, source_target_pairs={{0,16},{16,32},{32,48},{48,64},{64,80},{80,96},{96,112},{112,128},... | collective-permute-start | bytes 294920 | tf_op jit(solution)/shard_map/ppermute | solution.py:35
  35.8 2.2 copy-start.10
  41.4 33.5 %all-to-all-start = ((f32[64,1,2048]{2,1,0:T(1,128)}), f32[64,1,2048]{2,1,0:T(1,128)}, u32[]{:S(2)}, u32[]{:S(2)}) async-start(f32[64,1,2048]{2,1,0:T(1,128)} %reshape.170), calls=%async_computation | async-start | bytes 1048576 | tf_op jit(solution)/shard_map/all_to_all | solution.py:18
  124.1 2.5 %copy-start.7 = (f32[1,1,2,64,1152]{4,3,2,1,0:T(8,128)S(1)}, f32[1,1,2,64,1152]{4,3,2,1,0:T(8,128)}, u32[]{:S(2)}) copy-start(f32[1,1,2,64,1152]{4,3,2,1,0:T(8,128)} %param.6) | copy-start | bytes 1769476
  126.6 7.5 %copy-start.4 = (bf16[2,384,384]{2,1,0:T(8,128)(2,1)S(1)}, bf16[2,384,384]{2,1,0:T(8,128)(2,1)}, u32[]{:S(2)}) copy-start(bf16[2,384,384]{2,1,0:T(8,128)(2,1)} %copy-done.3) | copy-start | bytes 1769476
  126.7 12.6 %copy-start.2 = (bf16[2,384,384]{2,1,0:T(8,128)(2,1)S(1)}, bf16[2,384,384]{2,1,0:T(8,128)(2,1)}, u32[]{:S(2)}) copy-start(bf16[2,384,384]{2,1,0:T(8,128)(2,1)} %copy-done.1) | copy-start | bytes 1769476
  127.7 6.4 %collective-permute-start.6 = (bf16[2,64,192]{2,1,0:T(8,128)(2,1)}, bf16[2,64,192]{2,1,0:T(8,128)(2,1)}, u32[]{:S(2)}, u32[]{:S(2)}) collective-permute-start(bf16[2,64,192]{2,1,0:T(8,128)(2,1)} %bitcast.133), channel_id=1, source_target_pairs={{2,0},{4,2},{6,4},{8,6},{10,8},{12,10},{14,12},{3,1},{5,3},{7,5},{... | collective-permute-start | bytes 147464 | tf_op jit(solution)/shard_map/ppermute | solution.py:35
  132.1 7.2 %collective-permute-start.4 = (bf16[2,64,192]{2,1,0:T(8,128)(2,1)S(1)}, bf16[2,64,192]{2,1,0:T(8,128)(2,1)S(1)}, u32[]{:S(2)}, u32[]{:S(2)}) collective-permute-start(bf16[2,64,192]{2,1,0:T(8,128)(2,1)S(1)} %bitcast.155), channel_id=1, source_target_pairs={{16,0},{32,16},{48,32},{64,48},{80,64},{96,80},{112,96},{128,112},... | collective-permute-start | bytes 147464 | tf_op jit(solution)/shard_map/ppermute | solution.py:35
  139.9 6.4 %collective-permute-start.7 = (f32[2,64,192]{2,1,0:T(8,128)S(1)}, f32[2,64,192]{2,1,0:T(8,128)S(1)}, u32[]{:S(2)}, u32[]{:S(2)}) collective-permute-start(f32[2,64,192]{2,1,0:T(8,128)S(1)} %get-tuple-element.36), channel_id=1, source_target_pairs={{0,2},{2,4},{4,6},{6,8},{8,10},{10,12},{12,14},{1,3},{3,5},{5,7},{... | collective-permute-start | bytes 294920 | tf_op jit(solution)/shard_map/ppermute | solution.py:35
  142.9 6.3 %collective-permute-start.5 = (f32[2,64,192]{2,1,0:T(8,128)S(1)}, f32[2,64,192]{2,1,0:T(8,128)S(1)}, u32[]{:S(2)}, u32[]{:S(2)}) collective-permute-start(f32[2,64,192]{2,1,0:T(8,128)S(1)} %get-tuple-element.38), channel_id=1, source_target_pairs={{0,16},{16,32},{32,48},{48,64},{64,80},{80,96},{96,112},{112,128},... | collective-permute-start | bytes 294920 | tf_op jit(solution)/shard_map/ppermute | solution.py:35
  153.8 25.2 %all-to-all-start.5 = ((f32[64,1,2048]{2,1,0:T(1,128)}), f32[64,1,2048]{2,1,0:T(1,128)S(1)}, u32[]{:S(2)}, u32[]{:S(2)}) async-start(f32[64,1,2048]{2,1,0:T(1,128)} %reshape.174), calls=%async_computation.5 | async-start | bytes 1048576 | tf_op jit(solution)/shard_map/all_to_all | solution.py:18
where the time goes:
time: 227 us; the launch traced here: 224 us
  blocking collectives  57 us (25%)
  starting transfers between devices  53.9 us (24%)
  waiting for transfers between devices  40.7 us (18%)
  local copies, waits for them, and re-layouts  27.8 us (12%)
  matrix products  24.4 us (11%)
  other arithmetic  18.5 us (8%)
    all_to_all x6, blocking collectives, copy_for_each(): return lax.all_to_all(copies, axis, split_axis=0, concat_axis=0, tiled=True)  57 us
    all_to_all x3, waiting for transfers between devices, copy_for_each(): return lax.all_to_all(copies, axis, split_axis=0, concat_axis=0, tiled=True)  31.9 us
    all_to_all x3, starting transfers between devices, copy_for_each(): return lax.all_to_all(copies, axis, split_axis=0, concat_axis=0, tiled=True)  28.6 us
    ppermute x8, starting transfers between devices, shifted(): return lax.ppermute(block, axis, route)  25.4 us
    unnamed x44, local copies, waits for them, and re-layouts  19.2 us
    all_to_all x4, other arithmetic, copy_for_each(): return lax.all_to_all(copies, axis, split_axis=0, concat_axis=0, tiled=True)  14.9 us
    ppermute x8, waiting for transfers between devices, shifted(): return lax.ppermute(block, axis, route)  8.75 us
    dot_general x6, matrix products, complex_apply(): jnp.dot(flattened, real_part, preferred_element_type=jnp.float32)  8.39 us
  transfers between devices with their start and end apart: 11, of which 6 were waited for; matrix products, arithmetic and copies ran while one was open for 8% of the time, Pallas kernels for 0%

commit v1 on v0

v1 whole, which is shorter than its diff:
```python
import functools

import jax
import jax.numpy as jnp
from jax import lax
from jax.experimental import pallas as pl
from jax.experimental.pallas import tpu as pltpu
from jax.sharding import PartitionSpec as P

ITERS = 2
STEP_RATIO = 0.4
MESH = pl.DeviceIdType.MESH
F32 = jnp.float32
BF16 = jnp.bfloat16
HIGHEST = lax.Precision.HIGHEST


def dot(a, b, precision=None):
    return jnp.dot(a, b, preferred_element_type=F32, precision=precision)


def dot_nt(a, b, precision=None):
    return lax.dot_general(
        a, b, (((1,), (1,)), ((), ())), preferred_element_type=F32, precision=precision
    )


def dot_tn(a, b):
    return lax.dot_general(a, b, (((0,), (0,)), ((), ())), preferred_element_type=F32)


def split(x):
    high = x.astype(BF16)
    return high, (x - high.astype(F32)).astype(BF16)


def kernel(
    shape,
    lead_ref,
    src_hbm,
    imp_hbm,
    maps_hbm,
    basis_hbm,
    inv_hbm,
    out_ref,
    src,
    imp,
    maps,
    basis,
    inv,
    solver,
    inv_all,
    outgoing,
    face_in,
    ret_out,
    ret_in,
    updated,
    state,
    rows,
    rows_turned,
    product,
    proj_rows,
    basis_k,
    mapped_k,
    gathered,
    sum_z,
    sum_m,
    sum_c,
    load_sem,
    send_sem,
    recv_sem,
):
    nz, nh, ny, nc, ncol = shape
    nm = nh * ny
    ngx, ngy = nz * nh, ny * nc
    sources = src.shape[0] // 2
    trace = src.shape[1]
    face = trace // 6
    pair = 2 * face
    cps = basis.shape[0]
    half = cps // 2

    gx, gy, col = lax.axis_index("gx"), lax.axis_index("gy"), lax.axis_index("col")
    z, xh = gx // nh, gx % nh
    y, core = gy // nc, gy % nc
    m = xh * ny + y

    def at(z_to, m_to, core_to):
        return {
            "gx": z_to * nh + m_to // ny,
            "gy": (m_to % ny) * nc + core_to,
            "col": col,
        }

    z_peers = [at((z + o) % nz, m, core) for o in range(1, nz)]
    m_peers = [at(z, (m + o) % nm, core) for o in range(1, nm)]
    c_peers = [at(z, m, (core + o) % nc) for o in range(1, nc)]
    below = [
        {"gx": (gx + ngx - 1) % ngx, "gy": gy, "col": col},
        {"gx": gx, "gy": (gy + ngy - 1) % ngy, "col": col},
    ]
    above = [
        {"gx": (gx + 1) % ngx, "gy": gy, "col": col},
        {"gx": gx, "gy": (gy + 1) % ngy, "col": col},
    ]
    col_peer = {"gx": gx, "gy": gy, "col": (col + 1) % ncol}
    position, last = [gx, gy], [ngx - 1, ngy - 1]

    loads = [
        pltpu.make_async_copy(a, b, load_sem.at[i])
        for i, (a, b) in enumerate(
            [(src_hbm, src), (maps_hbm, maps), (basis_hbm, basis), (inv_hbm, inv), (imp_hbm, imp)]
        )
    ]
    for load in loads:
        load.start()

    barrier = pltpu.get_barrier_semaphore()
    partners = z_peers + m_peers + c_peers + below + above + [col_peer]
    for partner in partners:
        pl.semaphore_signal(barrier, inc=1, device_id=partner, device_id_type=MESH)

    sent = []

    def remote(source, target, device):
        k = len(sent)
        copy = pltpu.make_async_remote_copy(
            src_ref=source,
            dst_ref=target,
            send_sem=send_sem.at[k],
            recv_sem=recv_sem.at[k],
            device_id=device,
            device_id_type=MESH,
        )
        copy.start()
        sent.append(copy)
        return copy

    def arrive(copies):
        for copy in copies:
            copy.wait_recv()

    lane = lax.broadcasted_iota(jnp.int32, (2 * sources, 128), 1)
    small_lane = lax.broadcasted_iota(jnp.int32, (half, 128), 1)

    loads[0].wait()
    outgoing[...] = src[...].astype(BF16)
    pl.semaphore_wait(barrier, len(partners))

    def send_faces(it):
        return [
            remote(outgoing.at[:, pl.ds(d * pair, 256)], face_in.at[it, d], below[d])
            for d in range(2)
        ]

    def turned(x):
        return jnp.concatenate([-x[sources:], x[:sources]], axis=0)

    def exchange(it, coming):
        returned, own = [], []
        for d in range(2):
            coming[d].wait_recv()
            upper = face_in[it, d]
            here = outgoing[:, pl.ds(d * pair, pair)]
            middle = jnp.where(
                lane < 64, upper[:, 128:].astype(F32), here[:, 128:256].astype(F32)
            ).astype(BF16)
            x = jnp.concatenate([upper[:, :128], middle, here[:, 256:]], axis=1)
            solved = dot(x, solver[d, 0]) + dot(turned(x), solver[d, 1])
            ret_out[it, d] = solved[:, :256].astype(BF16)
            returned.append(remote(ret_out.at[it, d], ret_in.at[it, d], above[d]))
            own.append(jnp.where(position[d] < last[d], solved[:, 128:], 0.0))
        ends = outgoing[:, pl.ds(2 * pair, pair)].astype(F32)
        updated[:, pl.ds(2 * pair, pair)] = pltpu.roll(ends, face, 1)
        for d in range(2):
            returned[d].wait_recv()
            back = jnp.where(position[d] > 0, ret_in[it, d].astype(F32), 0.0)
            updated[:, pl.ds(d * pair, 128)] = back[:, :128]
            updated[:, pl.ds(d * pair + 128, 128)] = jnp.where(
                lane < 64, back[:, 128:], own[d][:, :128]
            )
            updated[:, pl.ds(d * pair + 256, 128)] = own[d][:, 128:]

    def project(defect):
        high, low = split(defect)
        first = dot_nt(proj_rows[...], high)
        second = dot_nt(proj_rows[pl.ds(0, 2 * cps), :], low)
        by_part = first[: 2 * cps] + first[2 * cps :] + second
        total = by_part[:cps] + pltpu.roll(by_part[cps:], sources, 1)
        return jnp.where(
            small_lane < 64, total[:half], pltpu.roll(total[half:], sources, 1)
        ).astype(BF16)

    def squares(defect):
        sq = defect * defect
        folded = sq[:, :128]
        for t in range(1, trace // 128):
            folded = folded + sq[:, 128 * t : 128 * (t + 1)]
        folded = folded[:sources] + folded[sources:]
        both = jnp.concatenate([folded, folded], axis=0)
        return dot_nt(jnp.ones((8, 128), F32), both, HIGHEST)

    def gather_z(it, packed):
        gathered[it, z, m, core] = packed
        block = gathered.at[it, z, m, core]
        return [remote(block, block, peer) for peer in z_peers]

    def gather_m(it, coming):
        arrive(coming)
        block = gathered.at[it, :, m, core]
        return [remote(block, block, peer) for peer in m_peers]

    def gather_c(it, coming):
        arrive(coming)
        block = gathered.at[it, :, :, core]
        arrive([remote(block, block, peer) for peer in c_peers])

    def coarse_of(it):
        whole = gathered[it].reshape(-1, 128)
        parts = dot(inv_all[...].reshape(2 * cps, whole.shape[0]), whole)
        return parts[:cps] + pltpu.roll(parts[cps:], sources, 1)

    def total_of(it, row):
        for buffer, index, peers in ((sum_z, z, z_peers), (sum_m, m, m_peers), (sum_c, core, c_peers)):
            buffer[it, index] = row
            arrive([remote(buffer.at[it, index], buffer.at[it, index], peer) for peer in peers])
            row = buffer[it, 0]
            for i in range(1, buffer.shape[1]):
                row = row + buffer[it, i]
        return row

    def stacked(coefficients):
        high, low = split(coefficients)
        return jnp.concatenate([high, low, high], axis=0)[:, :sources]

    def factor_of(total):
        factor = STEP_RATIO * jnp.sqrt(total / (pltpu.roll(total, sources, 1) + 1e-06))
        return factor[0:1]

    def stack_k(target, block):
        for c in range(2):
            high, low = split(block[c * cps : (c + 1) * cps])
            target[c, pl.ds(0, cps)] = high
            target[c, pl.ds(cps, cps)] = high
            target[c, pl.ds(2 * cps, cps)] = low

    faces = send_faces(0)

    loads[1].wait()
    for d in range(2):
        for c in range(2):
            stored = maps[2 * d + c].astype(F32)
            swapped = jnp.concatenate([stored[face:], stored[:face]], axis=0)
            swapped = pltpu.roll(swapped, face, 1)
            solver[d, c] = jnp.where(lead_ref[d] == 0, swapped, stored).astype(BF16)

    loads[2].wait()
    both = jnp.concatenate([basis[:, 0, :], basis[:, 1, :]], axis=0)
    high, low = split(both)
    proj_rows[pl.ds(0, 2 * cps), :] = high
    proj_rows[pl.ds(2 * cps, 2 * cps), :] = low
    stack_k(basis_k, both)
    base = 2 * sources
    for part, block in enumerate((high, low)):
        rows[pl.ds(base + part * 2 * cps, 2 * cps), :] = block
        rows_turned[pl.ds(base + part * 2 * cps, 2 * cps), :] = jnp.concatenate(
            [-block[cps:], block[:cps]], axis=0
        )
    gram = dot_nt(both[:cps], both[:cps], HIGHEST) + dot_nt(both[cps:], both[cps:], HIGHEST)

    loads[3].wait()
    here = lax.broadcasted_iota(jnp.int32, (256, 256), 0)
    there = lax.broadcasted_iota(jnp.int32, (256, 256), 1)
    wanted = ((here // half) % 2) * 128 + (here // cps) * half + here % half
    order = jnp.where(there == wanted, 1.0, 0.0).astype(BF16)
    for j in range(inv.shape[1] // 256):
        moved = dot(inv[:, 256 * j : 256 * (j + 1)].astype(BF16), order).astype(BF16)
        for h in range(2):
            inv_all[h, col, :, pl.ds(128 * j, 128)] = moved[:, 128 * h : 128 * (h + 1)]
    inverse_coming = remote(inv_all.at[:, col], inv_all.at[:, col], col_peer)

    exchange(0, faces)

    first_updated = updated[...]
    coming = gather_z(0, project(first_updated))
    first_squares = squares(first_updated)
    high = first_updated.astype(BF16)
    rows[pl.ds(0, base), :] = high
    rows_turned[pl.ds(0, base), :] = turned(high)
    loads[4].wait()
    for j in range(trace // 384):
        span = pl.ds(384 * j, 384)
        product[:, span] = dot(rows[...], imp[pl.ds(0, trace), span]) + dot(
            rows_turned[...], imp[pl.ds(trace, trace), span]
        )
    coming = gather_m(0, coming)
    mapped = product[pl.ds(base, 2 * cps), :] + product[pl.ds(base + 2 * cps, 2 * cps), :]
    stack_k(mapped_k, mapped)
    gather_c(0, coming)
    inverse_coming.wait_recv()

    def scaled_coarse(it, norm):
        coarse = coarse_of(it)
        energy = jnp.sum(coarse * dot(gram, coarse, HIGHEST), axis=0, keepdims=True)
        wide_lane = lax.broadcasted_iota(jnp.int32, (8, 128), 1)
        row = jnp.where(
            wide_lane < 64, norm, pltpu.roll(jnp.broadcast_to(energy, (8, 128)), sources, 1)
        )
        return stacked(coarse * factor_of(total_of(it, row)))

    scaled = scaled_coarse(0, first_squares)
    for copy in faces:
        copy.wait_send()
    for c in range(2):
        part = pl.ds(c * sources, sources)
        outgoing[part, :] = (
            product[part, :] + src[part, :] + dot_tn(scaled, mapped_k[c])
        ).astype(BF16)
    coming = send_faces(1)
    for c in range(2):
        part = pl.ds(c * sources, sources)
        state[part, :] = updated[part, :] + dot_tn(scaled, basis_k[c])
    exchange(1, coming)
    defect = updated[...] - state[...]
    coming = gather_z(1, project(defect))
    second_squares = squares(defect)
    coming = gather_m(1, coming)
    gather_c(1, coming)
    scaled = scaled_coarse(1, second_squares)
    for c in range(2):
        part = pl.ds(c * sources, sources)
        out_ref[part, :] = updated[part, :] + dot_tn(scaled, basis_k[c])
    for copy in sent[len(faces) :]:
        copy.wait_send()


def per_device(shape, sources, impedance, pair_maps, lead_side, coarse_basis, coarse_inverse):
    nz, nh, ny, nc, ncol = shape
    here, trace = sources.shape[3], sources.shape[4]
    pair = pair_maps.shape[-1]
    cps = coarse_basis.shape[2]
    size = coarse_inverse.shape[1]
    nm = nh * ny
    copies = 1 + ITERS * (4 + 2 * (nz - 1 + nm - 1 + nc - 1))
    hbm = pl.BlockSpec(memory_space=pl.ANY)
    out = pl.pallas_call(
        functools.partial(kernel, shape),
        out_shape=jax.ShapeDtypeStruct((2 * here, trace), F32),
        in_specs=[pl.BlockSpec(memory_space=pltpu.SMEM)] + [hbm] * 5,
        out_specs=pl.BlockSpec(memory_space=pltpu.VMEM),
        scratch_shapes=[
            pltpu.VMEM((2 * here, trace), F32),
            pltpu.VMEM((2 * trace, trace), BF16),
            pltpu.VMEM((4, pair, pair), BF16),
            pltpu.VMEM((cps, 2, trace), F32),
            pltpu.VMEM((cps // 2, size), F32),
            pltpu.VMEM((2, 2, pair, pair), BF16),
            pltpu.VMEM((2, ncol, cps // 2, size // 2), BF16),
            pltpu.VMEM((2 * here, trace), BF16),
            pltpu.VMEM((ITERS, 2, 2 * here, 256), BF16),
            pltpu.VMEM((ITERS, 2, 2 * here, 256), BF16),
            pltpu.VMEM((ITERS, 2, 2 * here, 256), BF16),
            pltpu.VMEM((2 * here, trace), F32),
            pltpu.VMEM((2 * here, trace), F32),
            pltpu.VMEM((2 * here + 4 * cps, trace), BF16),
            pltpu.VMEM((2 * here + 4 * cps, trace), BF16),
            pltpu.VMEM((2 * here + 4 * cps, trace), F32),
            pltpu.VMEM((4 * cps, trace), BF16),
            pltpu.VMEM((2, 3 * cps, trace), BF16),
            pltpu.VMEM((2, 3 * cps, trace), BF16),
            pltpu.VMEM((ITERS, nz, nm, nc, cps // 2, 128), BF16),
            pltpu.VMEM((ITERS, nz, 8, 128), F32),
            pltpu.VMEM((ITERS, nm, 8, 128), F32),
            pltpu.VMEM((ITERS, nc, 8, 128), F32),
            pltpu.SemaphoreType.DMA((5,)),
            pltpu.SemaphoreType.DMA((copies,)),
            pltpu.SemaphoreType.DMA((copies,)),
        ],
        compiler_params=pltpu.CompilerParams(
            collective_id=0, has_side_effects=True, vmem_limit_bytes=60 * 1024 * 1024
        ),
    )(
        lead_side.reshape(2),
        sources.reshape(2 * here, trace),
        impedance.reshape(2 * trace, trace),
        pair_maps.reshape(4, pair, pair),
        coarse_basis[0, 0],
        coarse_inverse,
    )
    return out.reshape(1, 1, 2, here, trace)


SHAPE = (8, 2, 4, 2, 2)


def build(mesh, shape):
    return jax.shard_map(
        functools.partial(per_device, shape),
        mesh=mesh,
        in_specs=(
            P("gx", "gy", None, "col", None),
            P("gx", "gy", None, None, None),
            P("gx", "gy", None, None, None, None),
            P("gx", "gy", None),
            P("gx", "gy", None, None, None),
            P(("gx", "gy", "col"), None),
        ),
        out_specs=P("gx", "gy", None, "col", None),
        check_vma=False,
    )


def solution(mesh):
    return build(mesh, SHAPE)
```

time: 227 us -> 81.2 us (0.36); the launches traced: 224 us -> 81.1 us
  Pallas kernels: 0 us -> 79.2 us
  blocking collectives: 57 us -> 0 us
  starting transfers between devices: 53.9 us -> 0 us
  waiting for transfers between devices: 40.7 us -> 0 us
  local copies, waits for them, and re-layouts: 27.8 us -> 1.92 us
  matrix products: 24.4 us -> 0 us
  other arithmetic: 18.5 us -> 0 us
    pallas_call x0 -> x1, Pallas kernels: none -> 79.2 us  [per_device(): pl.pallas_call(functools.partial(kernel, shape), out_shape=jax.ShapeDtype...]
    all_to_all x6 -> x0, blocking collectives: 57 us -> none  [copy_for_each(): return lax.all_to_all(copies, axis, split_axis=0, concat_axis=0, tiled=True)]
    all_to_all x3 -> x0, waiting for transfers between devices: 31.9 us -> none  [copy_for_each(): return lax.all_to_all(copies, axis, split_axis=0, concat_axis=0, tiled=True)]
    all_to_all x3 -> x0, starting transfers between devices: 28.6 us -> none  [copy_for_each(): return lax.all_to_all(copies, axis, split_axis=0, concat_axis=0, tiled=True)]
    ppermute x8 -> x0, starting transfers between devices: 25.4 us -> none  [shifted(): return lax.ppermute(block, axis, route)]
    dot_general x18 -> x0, matrix products: 24.4 us -> none  [the longest x6 8.39 us: complex_apply(): jnp.dot(flattened, real_part, preferred_element_type=jnp.float32)]
    unnamed x44 -> x1, local copies, waits for them, and re-layouts: 19.2 us -> 1.92 us
    all_to_all x4 -> x0, other arithmetic: 14.9 us -> none  [copy_for_each(): return lax.all_to_all(copies, axis, split_axis=0, concat_axis=0, tiled=True)]
  transfers between devices with their start and end apart: 11 -> 0, of which waited for: 6 -> 0; matrix products, arithmetic and copies ran while one was open for 8% -> 0% of each run, Pallas kernels for 0% -> 0%
where the time goes in v1:
time: 81.2 us; the launch traced here: 81.1 us
  Pallas kernels  79.2 us (98%)
  local copies, waits for them, and re-layouts  1.92 us (2%)
    pallas_call x1, Pallas kernels, per_device(): pl.pallas_call(functools.partial(kernel, shape), out_shape=jax.ShapeDtype...  79.2 us
    unnamed x1, local copies, waits for them, and re-layouts  1.92 us

profile of v1, /device:TPU:1, one launch (start us, length us, event | category | flops | bytes accessed | tf_op | source)
XLA Modules:
  0.0 81.1 jit_solution(5562366469749692639)
XLA Ops:
  0.0 79.2 %shard_map.64 = f32[128,1152]{1,0:T(8,128)} custom-call(s32[2]{0:T(128)} %bitcast.11, f32[128,1152]{1,0:T(8,128)} %bitcast.9, bf16[2304,1152]{1,0:T(8,128)(2,1)} %bitcast.6, bf16[4,384,384]{2,1,0:T(8,128)(2,1)} %bitcast.8, f32[32,2,1152]{2,1,0:T(2,128)} %bitcast.10, f32[16,4096]{1,0:T(8,128)} %inv_hbm.1), custom_call_target="tpu_custom_call" | custom-call | tf_op jit(solution)/shard_map/pallas_call | solution.py:346
  79.2 1.9 %copy.8 = f32[1,1,2,64,1152]{4,3,2,1,0:T(8,128)} copy(f32[1,1,2,64,1152]{4,3,2,1,0:T(8,128)} %bitcast.7) | data formatting | bytes 1179648

commit v2 on v1

v2 whole, which is shorter than its diff:
```python
import functools

import jax
import jax.numpy as jnp
from jax import lax
from jax.experimental import pallas as pl
from jax.experimental.pallas import tpu as pltpu
from jax.sharding import PartitionSpec as P

STEP_RATIO = 0.4
MESH = pl.DeviceIdType.MESH
F32 = jnp.float32
BF16 = jnp.bfloat16
HIGHEST = lax.Precision.HIGHEST


def dot(a, b, precision=None):
    return jnp.dot(a, b, preferred_element_type=F32, precision=precision)


def dot_nt(a, b, precision=None):
    return lax.dot_general(
        a, b, (((1,), (1,)), ((), ())), preferred_element_type=F32, precision=precision
    )


def dot_tn(a, b):
    return lax.dot_general(a, b, (((0,), (0,)), ((), ())), preferred_element_type=F32)


def split(x):
    high = x.astype(BF16)
    return high, (x - high.astype(F32)).astype(BF16)


def kernel(
    shape,
    lead_ref,
    src_hbm,
    imp_hbm,
    maps_hbm,
    basis_hbm,
    inv_hbm,
    out_ref,
    src,
    imp,
    maps,
    basis,
    inv,
    solver,
    inv_all,
    outgoing,
    image_out,
    face_in,
    image_in,
    ret_out,
    ret_in,
    solved_own,
    updated,
    state,
    rows,
    rows_turned,
    product,
    image,
    image_solved,
    proj_rows,
    basis_k,
    mapped,
    mapped_near,
    mapped_k,
    mapped_end,
    kernel_t,
    near_out,
    near_in,
    gathered,
    sum_z,
    sum_m,
    sum_c,
    load_sem,
    send_sem,
    recv_sem,
):
    nz, nh, ny, nc, ncol = shape
    nm = nh * ny
    ngx, ngy = nz * nh, ny * nc
    sources = src.shape[0] // 2
    trace = src.shape[1]
    face = trace // 6
    pair = 2 * face
    cps = basis.shape[0]
    half = cps // 2

    gx, gy, col = lax.axis_index("gx"), lax.axis_index("gy"), lax.axis_index("col")
    z, xh = gx // nh, gx % nh
    y, core = gy // nc, gy % nc
    m = xh * ny + y

    def at(z_to, m_to, core_to):
        return {
            "gx": z_to * nh + m_to // ny,
            "gy": (m_to % ny) * nc + core_to,
            "col": col,
        }

    z_peers = [at((z + o) % nz, m, core) for o in range(1, nz)]
    m_peers = [at(z, (m + o) % nm, core) for o in range(1, nm)]
    c_peers = [at(z, m, (core + o) % nc) for o in range(1, nc)]
    below = [
        {"gx": (gx + ngx - 1) % ngx, "gy": gy, "col": col},
        {"gx": gx, "gy": (gy + ngy - 1) % ngy, "col": col},
    ]
    above = [
        {"gx": (gx + 1) % ngx, "gy": gy, "col": col},
        {"gx": gx, "gy": (gy + 1) % ngy, "col": col},
    ]
    col_peer = {"gx": gx, "gy": gy, "col": (col + 1) % ncol}
    position, last = [gx, gy], [ngx - 1, ngy - 1]

    loads = [
        pltpu.make_async_copy(a, b, load_sem.at[i])
        for i, (a, b) in enumerate(
            [(src_hbm, src), (maps_hbm, maps), (basis_hbm, basis), (inv_hbm, inv), (imp_hbm, imp)]
        )
    ]
    for load in loads:
        load.start()

    barrier = pltpu.get_barrier_semaphore()
    partners = z_peers + m_peers + c_peers + below + above + [col_peer]
    for partner in partners:
        pl.semaphore_signal(barrier, inc=1, device_id=partner, device_id_type=MESH)

    sent = []

    def remote(source, target, device):
        k = len(sent)
        copy = pltpu.make_async_remote_copy(
            src_ref=source,
            dst_ref=target,
            send_sem=send_sem.at[k],
            recv_sem=recv_sem.at[k],
            device_id=device,
            device_id_type=MESH,
        )
        copy.start()
        sent.append(copy)
        return copy

    def arrive(copies):
        for copy in copies:
            copy.wait_recv()

    def lanes(n):
        return lax.broadcasted_iota(jnp.int32, (n, 128), 1)

    def turned(x):
        part = x.shape[0] // 2
        return jnp.concatenate([-x[part:], x[:part]], axis=0)

    def send_faces(it):
        return [
            remote(outgoing.at[it, :, pl.ds(d * pair, 256)], face_in.at[it, d], below[d])
            for d in range(2)
        ]

    def solve(it, d, coming):
        coming[d].wait_recv()
        upper = face_in[it, d]
        here = outgoing[it, :, pl.ds(d * pair, pair)]
        middle = jnp.where(
            lanes(2 * sources) < 64, upper[:, 128:].astype(F32), here[:, 128:256].astype(F32)
        ).astype(BF16)
        x = jnp.concatenate([upper[:, :128], middle, here[:, 256:]], axis=1)
        solved = dot(x, solver[d, 0]) + dot(turned(x), solver[d, 1])
        ret_out[it, d] = solved[:, :256].astype(BF16)
        solved_own[d] = solved[:, 128:]
        return remote(ret_out.at[it, d], ret_in.at[it, d], above[d])

    def assemble(it, returned):
        ends = outgoing[it, :, pl.ds(2 * pair, pair)].astype(F32)
        updated[it, :, pl.ds(2 * pair, pair)] = pltpu.roll(ends, face, 1)
        for d in range(2):
            returned[d].wait_recv()
            back = jnp.where(position[d] > 0, ret_in[it, d].astype(F32), 0.0)
            own = jnp.where(position[d] < last[d], solved_own[d], 0.0)
            updated[it, :, pl.ds(d * pair, 128)] = back[:, :128]
            updated[it, :, pl.ds(d * pair + 128, 128)] = jnp.where(
                lanes(2 * sources) < 64, back[:, 128:], own[:, :128]
            )
            updated[it, :, pl.ds(d * pair + 256, 128)] = own[:, 128:]

    def apply_map(j):
        span = pl.ds(384 * j, 384)
        return dot(rows[...], imp[pl.ds(0, trace), span]) + dot(
            rows_turned[...], imp[pl.ds(trace, trace), span]
        )

    def packed(total):
        return jnp.where(
            lanes(half) < 64, total[:half], pltpu.roll(total[half:], sources, 1)
        ).astype(BF16)

    def project(defect):
        high, low = split(defect)
        first = dot_nt(proj_rows[...], high)
        second = dot_nt(proj_rows[pl.ds(0, 2 * cps), :], low)
        by_part = first[: 2 * cps] + first[2 * cps :] + second
        return packed(by_part[:cps] + pltpu.roll(by_part[cps:], sources, 1))

    def source_sums(products):
        folded = products[:, :128]
        for t in range(1, trace // 128):
            folded = folded + products[:, 128 * t : 128 * (t + 1)]
        folded = folded[:sources] + folded[sources:]
        both = jnp.concatenate([folded, folded], axis=0)
        return dot_nt(jnp.ones((8, 128), F32), both, HIGHEST)

    def gather_z(it, block):
        gathered[it, z, m, core] = block
        own = gathered.at[it, z, m, core]
        return [remote(own, own, peer) for peer in z_peers]

    def gather_m(it, coming):
        arrive(coming)
        block = gathered.at[it, :, m, core]
        return [remote(block, block, peer) for peer in m_peers]

    def gather_c(it, coming):
        arrive(coming)
        block = gathered.at[it, :, :, core]
        return [remote(block, block, peer) for peer in c_peers]

    def coarse_of(it, coming):
        arrive(coming)
        whole = gathered[it].reshape(-1, 128)
        parts = dot(inv_all[...].reshape(2 * cps, whole.shape[0]), whole)
        return parts[:cps] + pltpu.roll(parts[cps:], sources, 1)

    def share(buffer, it, index, peers, row):
        buffer[it, index] = row
        own = buffer.at[it, index]
        return [remote(own, own, peer) for peer in peers]

    def added(buffer, it, coming):
        arrive(coming)
        row = buffer[it, 0]
        for i in range(1, buffer.shape[1]):
            row = row + buffer[it, i]
        return row

    def stacked(coefficients):
        high, low = split(coefficients)
        return jnp.concatenate([high, low, high], axis=0)[:, :sources]

    def factor_of(total):
        return STEP_RATIO * jnp.sqrt(total / (pltpu.roll(total, sources, 1) + 1e-06))

    def energy_of(coarse):
        energy = jnp.sum(coarse * dot(gram, coarse, HIGHEST), axis=0, keepdims=True)
        return pltpu.roll(jnp.broadcast_to(energy, (8, 128)), sources, 1)

    def three(block):
        high, low = split(block)
        return jnp.concatenate([high, high, low], axis=0)

    def mapped_sum(near, c, d):
        if d == 2:
            return dot_tn(stacked(near[0]), mapped_end[c])
        coefficients = jnp.concatenate(
            [stacked(near[0]), stacked(near[1 + 2 * d]), stacked(near[2 + 2 * d])], axis=0
        )
        return dot_tn(coefficients, mapped_k[c, d])

    loads[0].wait()
    outgoing[0] = src[...].astype(BF16)
    pl.semaphore_wait(barrier, len(partners))
    faces = send_faces(0)

    loads[1].wait()
    for d in range(2):
        for c in range(2):
            stored = maps[2 * d + c].astype(F32)
            swapped = jnp.concatenate([stored[face:], stored[:face]], axis=0)
            swapped = pltpu.roll(swapped, face, 1)
            solver[d, c] = jnp.where(lead_ref[d] == 0, swapped, stored).astype(BF16)
    loads[2].wait()
    both = jnp.concatenate([basis[:, 0, :], basis[:, 1, :]], axis=0)
    high, low = split(both)
    proj_rows[pl.ds(0, 2 * cps), :] = high
    proj_rows[pl.ds(2 * cps, 2 * cps), :] = low
    for part, block in enumerate((high, low)):
        rows[pl.ds(part * 2 * cps, 2 * cps), :] = block
        rows_turned[pl.ds(part * 2 * cps, 2 * cps), :] = turned(block)
    returned = [solve(0, d, faces) for d in range(2)]

    loads[4].wait()
    for j in range(trace // 384):
        whole = apply_map(j)
        whole = whole[: 2 * cps] + whole[2 * cps :]
        image[:, pl.ds(384 * j, 384)] = whole
        image_out[:, pl.ds(384 * j, 384)] = whole.astype(BF16)
    assemble(0, returned)

    coming = gather_z(0, project(updated[0]))
    image_coming = [
        remote(image_out.at[:, pl.ds(d * pair, 256)], image_in.at[d], below[d]) for d in range(2)
    ]
    high = updated[0].astype(BF16)
    rows[...] = high
    rows_turned[...] = turned(high)
    for j in range(trace // 384):
        span = pl.ds(384 * j, 384)
        outgoing[1, :, span] = (apply_map(j) + src[:, span]).astype(BF16)
    faces_next = send_faces(1)
    coming = gather_m(0, coming)

    loads[3].wait()
    here = lax.broadcasted_iota(jnp.int32, (256, 256), 0)
    there = lax.broadcasted_iota(jnp.int32, (256, 256), 1)
    wanted = ((here // half) % 2) * 128 + (here // cps) * half + here % half
    order = jnp.where(there == wanted, 1.0, 0.0).astype(BF16)
    for j in range(inv.shape[1] // 256):
        moved = dot(inv[:, 256 * j : 256 * (j + 1)].astype(BF16), order).astype(BF16)
        for h in range(2):
            inv_all[h, col, :, pl.ds(128 * j, 128)] = moved[:, 128 * h : 128 * (h + 1)]
    inverse_coming = remote(inv_all.at[:, col], inv_all.at[:, col], col_peer)

    image_returned = []
    for d in range(2):
        image_coming[d].wait_recv()
        upper = image_in[d].astype(F32)
        own = image_out[:, pl.ds(d * pair, pair)].astype(F32)
        low_lane = lanes(2 * cps) < 64
        zero = jnp.zeros((2 * cps, 128), F32)
        x = jnp.concatenate(
            [zero, jnp.where(low_lane, 0.0, own[:, 128:256]), own[:, 256:]], axis=1
        ).astype(BF16)
        w = jnp.concatenate(
            [upper[:, :128], jnp.where(low_lane, upper[:, 128:], 0.0), zero], axis=1
        ).astype(BF16)
        solved = dot(jnp.concatenate([x, w], axis=0), solver[d, 0]) + dot(
            jnp.concatenate([turned(x), turned(w)], axis=0), solver[d, 1]
        )
        ret_out[2, d] = solved[:, :256].astype(BF16)
        image_solved[d] = solved[:, 128:]
        image_returned.append(remote(ret_out.at[2, d], ret_in.at[2, d], above[d]))
    first_squares = source_sums(updated[0] * updated[0])
    gram = dot_nt(both[:cps], both[:cps], HIGHEST) + dot_nt(both[cps:], both[cps:], HIGHEST)
    for c in range(2):
        basis_k[c] = three(both[c * cps : (c + 1) * cps])
    returned = [solve(1, d, faces_next) for d in range(2)]
    coming = gather_c(0, coming)

    inverse_coming.wait_recv()
    coarse = coarse_of(0, coming)
    high, low = split(coarse)
    near_out[...] = jnp.where(
        lanes(cps) < 64, high.astype(F32), pltpu.roll(low.astype(F32), sources, 1)
    ).astype(BF16)
    near_coming = []
    for d in range(2):
        near_coming.append(remote(near_out, near_in.at[2 * d], above[d]))
        near_coming.append(remote(near_out, near_in.at[2 * d + 1], below[d]))
    first_row = jnp.where(lanes(8) < 64, first_squares, energy_of(coarse))

    assemble(1, returned)
    state[...] = updated[1] - updated[0]
    early = gather_z(2, project(state[...]))
    for d in range(2):
        image_returned[d].wait_recv()
        back = jnp.where(position[d] > 0, ret_in[2, d].astype(F32), 0.0)
        own = jnp.where(position[d] < last[d], image_solved[d], 0.0)
        for target, r, o in ((mapped, 2 * cps, 0), (mapped_near, 0, 2 * cps)):
            target[:, pl.ds(d * pair, 128)] = back[r : r + 2 * cps, :128]
            target[:, pl.ds(d * pair + 128, 128)] = jnp.where(
                lanes(2 * cps) < 64, back[r : r + 2 * cps, 128:], own[o : o + 2 * cps, :128]
            )
            target[:, pl.ds(d * pair + 256, 128)] = own[o : o + 2 * cps, 128:]
    mapped[:, pl.ds(2 * pair, pair)] = pltpu.roll(image[:, pl.ds(2 * pair, pair)], face, 1)
    moved = mapped[...] - both
    blocks = [
        dot_nt(moved[:cps], both[:cps], HIGHEST) + dot_nt(moved[cps:], both[cps:], HIGHEST)
    ]
    left = lax.broadcasted_iota(jnp.int32, (cps, pair), 1) < face
    for d in range(2):
        total = 0.0
        for c in range(2):
            part = mapped_near[pl.ds(c * cps, cps), pl.ds(d * pair, pair)]
            sides = jnp.concatenate([jnp.where(left, part, 0.0), jnp.where(left, 0.0, part)], axis=0)
            total = total + dot_nt(
                sides, both[c * cps : (c + 1) * cps, d * pair : (d + 1) * pair], HIGHEST
            )
            own = three(mapped[pl.ds(c * cps, cps), pl.ds(d * pair, pair)])
            mapped_k[c, d] = jnp.concatenate(
                [own, three(sides[:cps]), three(sides[cps:])], axis=0
            )
        blocks.append(total)
    for c in range(2):
        mapped_end[c] = three(mapped[pl.ds(c * cps, cps), pl.ds(2 * pair, pair)])
    kernel_t[...] = jnp.concatenate(blocks, axis=0).T

    arrive(near_coming)
    near = [coarse]
    for i in range(4):
        both_parts = near_in[i].astype(F32)
        near.append(both_parts + pltpu.roll(both_parts, sources, 1))
    late = gather_z(1, packed(dot(kernel_t[...], jnp.concatenate(near, axis=0), HIGHEST)))
    norms = share(sum_z, 0, z, z_peers, first_row)
    early = gather_m(2, early)
    for c in range(2):
        part = pl.ds(c * sources, sources)
        for d in range(3):
            product[part, pl.ds(d * pair, pair)] = mapped_sum(near, c, d)
        product[part, :] = product[part, :] - dot_tn(stacked(coarse), basis_k[c])
    late = gather_m(1, late)
    norms = share(sum_m, 0, m, m_peers, added(sum_z, 0, norms))
    sums_aa = source_sums(state[...] * state[...])
    sums_ab = source_sums(state[...] * product[...])
    sums_bb = source_sums(product[...] * product[...])
    early = gather_c(2, early)
    coarse_early = coarse_of(2, early)
    late = gather_c(1, late)
    norms = share(sum_c, 0, core, c_peers, added(sum_m, 0, norms))
    factor = factor_of(added(sum_c, 0, norms))
    coarse = coarse_early + factor[0:1] * coarse_of(1, late)
    squares = sums_aa + factor * (2.0 * sums_ab + factor * sums_bb)
    row = jnp.where(lanes(8) < 64, squares, energy_of(coarse))
    norms = share(sum_z, 1, z, z_peers, row)
    near = [factor[0:1] * part for part in near]
    for c in range(2):
        part = pl.ds(c * sources, sources)
        for d in range(3):
            span = pl.ds(d * pair, pair)
            updated[1, part, span] = updated[1, part, span] + mapped_sum(near, c, d)
    norms = share(sum_m, 1, m, m_peers, added(sum_z, 1, norms))
    norms = share(sum_c, 1, core, c_peers, added(sum_m, 1, norms))
    factor = factor_of(added(sum_c, 1, norms))
    scaled = stacked(factor[0:1] * coarse)
    for c in range(2):
        part = pl.ds(c * sources, sources)
        out_ref[part, :] = updated[1, part, :] + dot_tn(scaled, basis_k[c])
    for copy in sent:
        copy.wait_send()


def per_device(shape, sources, impedance, pair_maps, lead_side, coarse_basis, coarse_inverse):
    nz, nh, ny, nc, ncol = shape
    here, trace = sources.shape[3], sources.shape[4]
    pair = pair_maps.shape[-1]
    cps = coarse_basis.shape[2]
    size = coarse_inverse.shape[1]
    nm = nh * ny
    copies = 1 + 3 * 4 + 4 + 5 * (nz - 1 + nm - 1 + nc - 1)
    hbm = pl.BlockSpec(memory_space=pl.ANY)
    out = pl.pallas_call(
        functools.partial(kernel, shape),
        out_shape=jax.ShapeDtypeStruct((2 * here, trace), F32),
        in_specs=[pl.BlockSpec(memory_space=pltpu.SMEM)] + [hbm] * 5,
        out_specs=pl.BlockSpec(memory_space=pltpu.VMEM),
        scratch_shapes=[
            pltpu.VMEM((2 * here, trace), F32),
            pltpu.VMEM((2 * trace, trace), BF16),
            pltpu.VMEM((4, pair, pair), BF16),
            pltpu.VMEM((cps, 2, trace), F32),
            pltpu.VMEM((cps // 2, size), F32),
            pltpu.VMEM((2, 2, pair, pair), BF16),
            pltpu.VMEM((2, ncol, cps // 2, size // 2), BF16),
            pltpu.VMEM((2, 2 * here, trace), BF16),
            pltpu.VMEM((2 * cps, trace), BF16),
            pltpu.VMEM((2, 2, 2 * here, 256), BF16),
            pltpu.VMEM((2, 2 * cps, 256), BF16),
            pltpu.VMEM((3, 2, 2 * here, 256), BF16),
            pltpu.VMEM((3, 2, 2 * here, 256), BF16),
            pltpu.VMEM((2, 2 * here, 256), F32),
            pltpu.VMEM((2, 2 * here, trace), F32),
            pltpu.VMEM((2 * here, trace), F32),
            pltpu.VMEM((2 * here, trace), BF16),
            pltpu.VMEM((2 * here, trace), BF16),
            pltpu.VMEM((2 * here, trace), F32),
            pltpu.VMEM((2 * cps, trace), F32),
            pltpu.VMEM((2, 4 * cps, 256), F32),
            pltpu.VMEM((4 * cps, trace), BF16),
            pltpu.VMEM((2, 3 * cps, trace), BF16),
            pltpu.VMEM((2 * cps, trace), F32),
            pltpu.VMEM((2 * cps, 2 * pair), F32),
            pltpu.VMEM((2, 2, 9 * cps, pair), BF16),
            pltpu.VMEM((2, 3 * cps, pair), BF16),
            pltpu.VMEM((cps, 5 * cps), F32),
            pltpu.VMEM((cps, 128), BF16),
            pltpu.VMEM((4, cps, 128), BF16),
            pltpu.VMEM((3, nz, nm, nc, cps // 2, 128), BF16),
            pltpu.VMEM((2, nz, 8, 128), F32),
            pltpu.VMEM((2, nm, 8, 128), F32),
            pltpu.VMEM((2, nc, 8, 128), F32),
            pltpu.SemaphoreType.DMA((5,)),
            pltpu.SemaphoreType.DMA((copies,)),
            pltpu.SemaphoreType.DMA((copies,)),
        ],
        compiler_params=pltpu.CompilerParams(
            collective_id=0, has_side_effects=True, vmem_limit_bytes=60 * 1024 * 1024
        ),
    )(
        lead_side.reshape(2),
        sources.reshape(2 * here, trace),
        impedance.reshape(2 * trace, trace),
        pair_maps.reshape(4, pair, pair),
        coarse_basis[0, 0],
        coarse_inverse,
    )
    return out.reshape(1, 1, 2, here, trace)


SHAPE = (8, 2, 4, 2, 2)


def build(mesh, shape):
    return jax.shard_map(
        functools.partial(per_device, shape),
        mesh=mesh,
        in_specs=(
            P("gx", "gy", None, "col", None),
            P("gx", "gy", None, None, None),
            P("gx", "gy", None, None, None, None),
            P("gx", "gy", None),
            P("gx", "gy", None, None, None),
            P(("gx", "gy", "col"), None),
        ),
        out_specs=P("gx", "gy", None, "col", None),
        check_vma=False,
    )


def solution(mesh):
    return build(mesh, SHAPE)
```

time: 81.2 us -> 66.9 us (0.82)
  Pallas kernels: 79.2 us -> 64.9 us
    pallas_call x1, Pallas kernels: 79.2 us -> 64.9 us  [per_device(): pl.pallas_call(functools.partial(kernel, shape), out_shape=jax.ShapeDtype...]
where the time goes in v2:
time: 66.9 us; the launch traced here: 66.8 us
  Pallas kernels  64.9 us (97%)
  local copies, waits for them, and re-layouts  1.92 us (3%)
    pallas_call x1, Pallas kernels, per_device(): pl.pallas_call(functools.partial(kernel, shape), out_shape=jax.ShapeDtype...  64.9 us
    unnamed x1, local copies, waits for them, and re-layouts  1.92 us

profile of v2, /device:TPU:1, one launch (start us, length us, event | category | flops | bytes accessed | tf_op | source)
XLA Modules:
  0.0 66.8 jit_solution(13797001776079162960)
XLA Ops:
  0.0 64.9 %shard_map.64 = f32[128,1152]{1,0:T(8,128)} custom-call(s32[2]{0:T(128)} %bitcast.11, f32[128,1152]{1,0:T(8,128)} %bitcast.9, bf16[2304,1152]{1,0:T(8,128)(2,1)} %bitcast.6, bf16[4,384,384]{2,1,0:T(8,128)(2,1)} %bitcast.8, f32[32,2,1152]{2,1,0:T(2,128)} %bitcast.10, f32[16,4096]{1,0:T(8,128)} %inv_hbm.1), custom_call_target="tpu_custom_call" | custom-call | tf_op jit(solution)/shard_map/pallas_call | solution.py:455
  64.9 1.9 %copy.8 = f32[1,1,2,64,1152]{4,3,2,1,0:T(8,128)} copy(f32[1,1,2,64,1152]{4,3,2,1,0:T(8,128)} %bitcast.7) | data formatting | bytes 1179648

commit v3 on v2

--- a/solution.py
+++ b/solution.py
@@ -74,8 +74,7 @@
     near_in,
     gathered,
     sum_z,
-    sum_m,
-    sum_c,
+    sum_q,
     load_sem,
     send_sem,
     recv_sem,
@@ -105,6 +104,13 @@
     z_peers = [at((z + o) % nz, m, core) for o in range(1, nz)]
     m_peers = [at(z, (m + o) % nm, core) for o in range(1, nm)]
     c_peers = [at(z, m, (core + o) % nc) for o in range(1, nc)]
+    q, nq = m * nc + core, nm * nc
+    q_peers = [at(z, (q + o) % nq // nc, (q + o) % nq % nc) for o in range(1, nq)]
+    offsets = [0]
+    for o in range(1, nz // 2 + 1):
+        offsets += [o] if 2 * o == nz else [o, nz - o]
+    bounds = [0, 1] + list(range(3, nz - 2, 2)) + ([nz] if nz > 1 else [])
+    groups = list(zip(bounds, bounds[1:]))
     below = [
         {"gx": (gx + ngx - 1) % ngx, "gy": gy, "col": col},
         {"gx": gx, "gy": (gy + ngy - 1) % ngy, "col": col},
@@ -122,13 +128,14 @@
             [(src_hbm, src), (maps_hbm, maps), (basis_hbm, basis), (inv_hbm, inv), (imp_hbm, imp)]
         )
     ]
-    for load in loads:
-        load.start()
+    loads[0].start()
 
     barrier = pltpu.get_barrier_semaphore()
-    partners = z_peers + m_peers + c_peers + below + above + [col_peer]
+    partners = below + above + z_peers + q_peers + [col_peer]
     for partner in partners:
         pl.semaphore_signal(barrier, inc=1, device_id=partner, device_id_type=MESH)
+    for i in (3, 1, 2, 4):
+        loads[i].start()
 
     sent = []
 
@@ -215,25 +222,34 @@
         both = jnp.concatenate([folded, folded], axis=0)
         return dot_nt(jnp.ones((8, 128), F32), both, HIGHEST)
 
-    def gather_z(it, block):
-        gathered[it, z, m, core] = block
-        own = gathered.at[it, z, m, core]
-        return [remote(own, own, peer) for peer in z_peers]
-
-    def gather_m(it, coming):
+    def forward(it, low, high):
+        block = gathered.at[it, pl.ds(low, high - low), m, core]
+        return [remote(block, block, peer) for peer in m_peers]
+
+    def gather_start(it, block):
+        gathered[it, 0, m, core] = block
+        own = gathered.at[it, 0, m, core]
+        coming = [None]
+        for i in range(1, nz):
+            coming.append(remote(own, gathered.at[it, i, m, core], z_peers[offsets[i] - 1]))
+        return coming
+
+    def gather_group(it, coming, low, high):
+        arrive(coming[max(low, 1) : high])
+        return forward(it, low, high)
+
+    def gather_core(it, coming, low, high):
         arrive(coming)
-        block = gathered.at[it, :, m, core]
-        return [remote(block, block, peer) for peer in m_peers]
-
-    def gather_c(it, coming):
-        arrive(coming)
-        block = gathered.at[it, :, :, core]
+        block = gathered.at[it, pl.ds(low, high - low), :, core]
         return [remote(block, block, peer) for peer in c_peers]
 
     def coarse_of(it, coming):
         arrive(coming)
-        whole = gathered[it].reshape(-1, 128)
-        parts = dot(inv_all[...].reshape(2 * cps, whole.shape[0]), whole)
+        parts = 0.0
+        for i in range(nz):
+            parts = parts + dot(
+                inv_all[i].reshape(2 * cps, nq * half), gathered[it, i].reshape(nq * half, 128)
+            )
         return parts[:cps] + pltpu.roll(parts[cps:], sources, 1)
 
     def share(buffer, it, index, peers, row):
@@ -276,6 +292,20 @@
     pl.semaphore_wait(barrier, len(partners))
     faces = send_faces(0)
 
+    loads[3].wait()
+    here = lax.broadcasted_iota(jnp.int32, (256, 256), 0)
+    there = lax.broadcasted_iota(jnp.int32, (256, 256), 1)
+    wanted = ((here // half) % 2) * 128 + (here // cps) * half + here % half
+    order = jnp.where(there == wanted, 1.0, 0.0).astype(BF16)
+    chunks = nq * cps // 256
+    for i in range(nz):
+        source_z = (z + nz - offsets[i]) % nz
+        for j in range(chunks):
+            start = pl.multiple_of((source_z * chunks + j) * 256, 256)
+            moved = dot(inv[:, pl.ds(start, 256)].astype(BF16), order).astype(BF16)
+            for h in range(2):
+                inv_all[i, h, col, :, pl.ds(128 * j, 128)] = moved[:, 128 * h : 128 * (h + 1)]
+    inverse_coming = remote(inv_all.at[:, :, col], inv_all.at[:, :, col], col_peer)
     loads[1].wait()
     for d in range(2):
         for c in range(2):
@@ -301,7 +331,8 @@
         image_out[:, pl.ds(384 * j, 384)] = whole.astype(BF16)
     assemble(0, returned)
 
-    coming = gather_z(0, project(updated[0]))
+    coming = gather_start(0, project(updated[0]))
+    moving = [gather_group(0, coming, *groups[0])]
     image_coming = [
         remote(image_out.at[:, pl.ds(d * pair, 256)], image_in.at[d], below[d]) for d in range(2)
     ]
@@ -311,19 +342,9 @@
     for j in range(trace // 384):
         span = pl.ds(384 * j, 384)
         outgoing[1, :, span] = (apply_map(j) + src[:, span]).astype(BF16)
+        if j + 1 < len(groups):
+            moving.append(gather_group(0, coming, *groups[j + 1]))
     faces_next = send_faces(1)
-    coming = gather_m(0, coming)
-
-    loads[3].wait()
-    here = lax.broadcasted_iota(jnp.int32, (256, 256), 0)
-    there = lax.broadcasted_iota(jnp.int32, (256, 256), 1)
-    wanted = ((here // half) % 2) * 128 + (here // cps) * half + here % half
-    order = jnp.where(there == wanted, 1.0, 0.0).astype(BF16)
-    for j in range(inv.shape[1] // 256):
-        moved = dot(inv[:, 256 * j : 256 * (j + 1)].astype(BF16), order).astype(BF16)
-        for h in range(2):
-            inv_all[h, col, :, pl.ds(128 * j, 128)] = moved[:, 128 * h : 128 * (h + 1)]
-    inverse_coming = remote(inv_all.at[:, col], inv_all.at[:, col], col_peer)
 
     image_returned = []
     for d in range(2):
@@ -348,8 +369,10 @@
     gram = dot_nt(both[:cps], both[:cps], HIGHEST) + dot_nt(both[cps:], both[cps:], HIGHEST)
     for c in range(2):
         basis_k[c] = three(both[c * cps : (c + 1) * cps])
+    split_at = groups[-1][0]
+    coming = gather_core(0, sum(moving[:-1], []), 0, split_at)
     returned = [solve(1, d, faces_next) for d in range(2)]
-    coming = gather_c(0, coming)
+    coming += gather_core(0, moving[-1], split_at, nz)
 
     inverse_coming.wait_recv()
     coarse = coarse_of(0, coming)
@@ -365,7 +388,7 @@
 
     assemble(1, returned)
     state[...] = updated[1] - updated[0]
-    early = gather_z(2, project(state[...]))
+    early = gather_start(2, project(state[...]))
     for d in range(2):
         image_returned[d].wait_recv()
         back = jnp.where(position[d] > 0, ret_in[2, d].astype(F32), 0.0)
@@ -404,24 +427,30 @@
     for i in range(4):
         both_parts = near_in[i].astype(F32)
         near.append(both_parts + pltpu.roll(both_parts, sources, 1))
-    late = gather_z(1, packed(dot(kernel_t[...], jnp.concatenate(near, axis=0), HIGHEST)))
+    coming = gather_start(
+        1, packed(dot(kernel_t[...], jnp.concatenate(near, axis=0), HIGHEST))
+    )
     norms = share(sum_z, 0, z, z_peers, first_row)
-    early = gather_m(2, early)
+    moving = [gather_group(1, coming, *groups[0])]
+    early = gather_group(2, early, 0, nz)
     for c in range(2):
         part = pl.ds(c * sources, sources)
         for d in range(3):
             product[part, pl.ds(d * pair, pair)] = mapped_sum(near, c, d)
         product[part, :] = product[part, :] - dot_tn(stacked(coarse), basis_k[c])
-    late = gather_m(1, late)
-    norms = share(sum_m, 0, m, m_peers, added(sum_z, 0, norms))
+        if c + 1 < len(groups):
+            moving.append(gather_group(1, coming, *groups[c + 1]))
+    for group in groups[3:]:
+        moving.append(gather_group(1, coming, *group))
+    norms = share(sum_q, 0, q, q_peers, added(sum_z, 0, norms))
     sums_aa = source_sums(state[...] * state[...])
     sums_ab = source_sums(state[...] * product[...])
     sums_bb = source_sums(product[...] * product[...])
-    early = gather_c(2, early)
+    early = gather_core(2, early, 0, nz)
+    late = gather_core(1, sum(moving[:-1], []), 0, split_at)
     coarse_early = coarse_of(2, early)
-    late = gather_c(1, late)
-    norms = share(sum_c, 0, core, c_peers, added(sum_m, 0, norms))
-    factor = factor_of(added(sum_c, 0, norms))
+    late += gather_core(1, moving[-1], split_at, nz)
+    factor = factor_of(added(sum_q, 0, norms))
     coarse = coarse_early + factor[0:1] * coarse_of(1, late)
     squares = sums_aa + factor * (2.0 * sums_ab + factor * sums_bb)
     row = jnp.where(lanes(8) < 64, squares, energy_of(coarse))
@@ -432,9 +461,8 @@
         for d in range(3):
             span = pl.ds(d * pair, pair)
             updated[1, part, span] = updated[1, part, span] + mapped_sum(near, c, d)
-    norms = share(sum_m, 1, m, m_peers, added(sum_z, 1, norms))
-    norms = share(sum_c, 1, core, c_peers, added(sum_m, 1, norms))
-    factor = factor_of(added(sum_c, 1, norms))
+    norms = share(sum_q, 1, q, q_peers, added(sum_z, 1, norms))
+    factor = factor_of(added(sum_q, 1, norms))
     scaled = stacked(factor[0:1] * coarse)
     for c in range(2):
         part = pl.ds(c * sources, sources)
@@ -450,8 +478,9 @@
     cps = coarse_basis.shape[2]
     size = coarse_inverse.shape[1]
     nm = nh * ny
-    copies = 1 + 3 * 4 + 4 + 5 * (nz - 1 + nm - 1 + nc - 1)
-    hbm = pl.BlockSpec(memory_space=pl.ANY)
+    copies = 1 + 3 * 4 + 4 + 3 * (nz - 1) + 9 * (nm - 1) + 5 * (nc - 1)
+    copies += 2 * (nz - 1 + nm * nc - 1)
+    hbm = pl.BlockSpec(memory_space=pltpu.HBM)
     out = pl.pallas_call(
         functools.partial(kernel, shape),
         out_shape=jax.ShapeDtypeStruct((2 * here, trace), F32),
@@ -464,7 +493,7 @@
             pltpu.VMEM((cps, 2, trace), F32),
             pltpu.VMEM((cps // 2, size), F32),
             pltpu.VMEM((2, 2, pair, pair), BF16),
-            pltpu.VMEM((2, ncol, cps // 2, size // 2), BF16),
+            pltpu.VMEM((nz, 2, ncol, cps // 2, nm * nc * cps // 2), BF16),
             pltpu.VMEM((2, 2 * here, trace), BF16),
             pltpu.VMEM((2 * cps, trace), BF16),
             pltpu.VMEM((2, 2, 2 * here, 256), BF16),
@@ -490,8 +519,7 @@
             pltpu.VMEM((4, cps, 128), BF16),
             pltpu.VMEM((3, nz, nm, nc, cps // 2, 128), BF16),
             pltpu.VMEM((2, nz, 8, 128), F32),
-            pltpu.VMEM((2, nm, 8, 128), F32),
-            pltpu.VMEM((2, nc, 8, 128), F32),
+            pltpu.VMEM((2, nm * nc, 8, 128), F32),
             pltpu.SemaphoreType.DMA((5,)),
             pltpu.SemaphoreType.DMA((copies,)),
             pltpu.SemaphoreType.DMA((copies,)),

time: 66.9 us -> 69.1 us (1.033)
  Pallas kernels: 64.9 us -> 67 us
    pallas_call x1, Pallas kernels: 64.9 us -> 67 us  [per_device(): pl.pallas_call(functools.partial(kernel, shape), out_shape=jax.ShapeDtype...]
where the time goes in v3:
time: 69.1 us; the launch traced here: 68.9 us
  Pallas kernels  67 us (97%)
  local copies, waits for them, and re-layouts  1.92 us (3%)
    pallas_call x1, Pallas kernels, per_device(): pl.pallas_call(functools.partial(kernel, shape), out_shape=jax.ShapeDtype...  67 us
    unnamed x1, local copies, waits for them, and re-layouts  1.92 us

profile of v3, /device:TPU:1, one launch (start us, length us, event | category | flops | bytes accessed | tf_op | source)
XLA Modules:
  0.0 68.9 jit_solution(1778787626239858987)
XLA Ops:
  0.0 67.0 %shard_map.64 = f32[128,1152]{1,0:T(8,128)} custom-call(s32[2]{0:T(128)} %bitcast.11, f32[128,1152]{1,0:T(8,128)} %bitcast.9, bf16[2304,1152]{1,0:T(8,128)(2,1)} %bitcast.6, bf16[4,384,384]{2,1,0:T(8,128)(2,1)} %bitcast.8, f32[32,2,1152]{2,1,0:T(2,128)} %bitcast.10, f32[16,4096]{1,0:T(8,128)} %inv_hbm.1), custom_call_target="tpu_custom_call" | custom-call | tf_op jit(solution)/shard_map/pallas_call | solution.py:484
  67.0 1.9 %copy.8 = f32[1,1,2,64,1152]{4,3,2,1,0:T(8,128)} copy(f32[1,1,2,64,1152]{4,3,2,1,0:T(8,128)} %bitcast.7) | data formatting | bytes 1179648

commit v4 on v3

--- a/solution.py
+++ b/solution.py
@@ -51,6 +51,7 @@
     inv_all,
     outgoing,
     image_out,
+    face_out,
     face_in,
     image_in,
     ret_out,
@@ -164,22 +165,30 @@
         part = x.shape[0] // 2
         return jnp.concatenate([-x[part:], x[:part]], axis=0)
 
-    def send_faces(it):
-        return [
-            remote(outgoing.at[it, :, pl.ds(d * pair, 256)], face_in.at[it, d], below[d])
-            for d in range(2)
-        ]
+    def packed_face(x):
+        part = x.shape[0] // 2
+        tail = jnp.where(
+            lanes(part) < 64, x[:part, 128:256], pltpu.roll(x[part:, 128:256], 64, 1)
+        )
+        return jnp.concatenate([x[:, :128], tail], axis=0).astype(BF16)
+
+    def face_parts(x):
+        size = 2 * x.shape[0] // 3
+        tail = x[size:].astype(F32)
+        return x[:size].astype(F32), jnp.concatenate([tail, pltpu.roll(tail, 64, 1)], axis=0)
+
+    def send_face(it, d):
+        face_out[it, d] = packed_face(outgoing[it, :, pl.ds(d * pair, 256)].astype(F32))
+        return remote(face_out.at[it, d], face_in.at[it, d], below[d])
 
     def solve(it, d, coming):
         coming[d].wait_recv()
-        upper = face_in[it, d]
+        head, tail = face_parts(face_in[it, d])
         here = outgoing[it, :, pl.ds(d * pair, pair)]
-        middle = jnp.where(
-            lanes(2 * sources) < 64, upper[:, 128:].astype(F32), here[:, 128:256].astype(F32)
-        ).astype(BF16)
-        x = jnp.concatenate([upper[:, :128], middle, here[:, 256:]], axis=1)
+        middle = jnp.where(lanes(2 * sources) < 64, tail, here[:, 128:256].astype(F32))
+        x = jnp.concatenate([head.astype(BF16), middle.astype(BF16), here[:, 256:]], axis=1)
         solved = dot(x, solver[d, 0]) + dot(turned(x), solver[d, 1])
-        ret_out[it, d] = solved[:, :256].astype(BF16)
+        ret_out[it, d] = packed_face(solved)
         solved_own[d] = solved[:, 128:]
         return remote(ret_out.at[it, d], ret_in.at[it, d], above[d])
 
@@ -188,11 +197,11 @@
         updated[it, :, pl.ds(2 * pair, pair)] = pltpu.roll(ends, face, 1)
         for d in range(2):
             returned[d].wait_recv()
-            back = jnp.where(position[d] > 0, ret_in[it, d].astype(F32), 0.0)
+            head, tail = face_parts(ret_in[it, d])
             own = jnp.where(position[d] < last[d], solved_own[d], 0.0)
-            updated[it, :, pl.ds(d * pair, 128)] = back[:, :128]
+            updated[it, :, pl.ds(d * pair, 128)] = jnp.where(position[d] > 0, head, 0.0)
             updated[it, :, pl.ds(d * pair + 128, 128)] = jnp.where(
-                lanes(2 * sources) < 64, back[:, 128:], own[:, :128]
+                lanes(2 * sources) < 64, jnp.where(position[d] > 0, tail, 0.0), own[:, :128]
             )
             updated[it, :, pl.ds(d * pair + 256, 128)] = own[:, 128:]
 
@@ -253,7 +262,7 @@
         return parts[:cps] + pltpu.roll(parts[cps:], sources, 1)
 
     def share(buffer, it, index, peers, row):
-        buffer[it, index] = row
+        buffer[it, index] = row[0:1]
         own = buffer.at[it, index]
         return [remote(own, own, peer) for peer in peers]
 
@@ -262,7 +271,7 @@
         row = buffer[it, 0]
         for i in range(1, buffer.shape[1]):
             row = row + buffer[it, i]
-        return row
+        return jnp.broadcast_to(row, (8, 128))
 
     def stacked(coefficients):
         high, low = split(coefficients)
@@ -290,7 +299,38 @@
     loads[0].wait()
     outgoing[0] = src[...].astype(BF16)
     pl.semaphore_wait(barrier, len(partners))
-    faces = send_faces(0)
+    faces = [send_face(0, d) for d in range(2)]
+
+    loads[2].wait()
+    both = jnp.concatenate([basis[:, 0, :], basis[:, 1, :]], axis=0)
+    high, low = split(both)
+    proj_rows[pl.ds(0, 2 * cps), :] = high
+    proj_rows[pl.ds(2 * cps, 2 * cps), :] = low
+    for part, block in enumerate((high, low)):
+        rows[pl.ds(part * 2 * cps, 2 * cps), :] = block
+        rows_turned[pl.ds(part * 2 * cps, 2 * cps), :] = turned(block)
+
+    loads[4].wait()
+
+    def apply_to_basis(j):
+        whole = apply_map(j)
+        whole = whole[: 2 * cps] + whole[2 * cps :]
+        image[:, pl.ds(384 * j, 384)] = whole
+        return whole
+
+    image_coming = []
+    for j in range(2):
+        image_out[j] = packed_face(apply_to_basis(j))
+        image_coming.append(remote(image_out.at[j], image_in.at[j], below[j]))
+    loads[1].wait()
+    for d in range(2):
+        for c in range(2):
+            stored = maps[2 * d + c].astype(F32)
+            swapped = jnp.concatenate([stored[face:], stored[:face]], axis=0)
+            swapped = pltpu.roll(swapped, face, 1)
+            solver[d, c] = jnp.where(lead_ref[d] == 0, swapped, stored).astype(BF16)
+    returned = [solve(0, d, faces) for d in range(2)]
+    apply_to_basis(2)
 
     loads[3].wait()
     here = lax.broadcasted_iota(jnp.int32, (256, 256), 0)
@@ -305,93 +345,51 @@
             moved = dot(inv[:, pl.ds(start, 256)].astype(BF16), order).astype(BF16)
             for h in range(2):
                 inv_all[i, h, col, :, pl.ds(128 * j, 128)] = moved[:, 128 * h : 128 * (h + 1)]
-    inverse_coming = remote(inv_all.at[:, :, col], inv_all.at[:, :, col], col_peer)
-    loads[1].wait()
-    for d in range(2):
-        for c in range(2):
-            stored = maps[2 * d + c].astype(F32)
-            swapped = jnp.concatenate([stored[face:], stored[:face]], axis=0)
-            swapped = pltpu.roll(swapped, face, 1)
-            solver[d, c] = jnp.where(lead_ref[d] == 0, swapped, stored).astype(BF16)
-    loads[2].wait()
-    both = jnp.concatenate([basis[:, 0, :], basis[:, 1, :]], axis=0)
-    high, low = split(both)
-    proj_rows[pl.ds(0, 2 * cps), :] = high
-    proj_rows[pl.ds(2 * cps, 2 * cps), :] = low
-    for part, block in enumerate((high, low)):
-        rows[pl.ds(part * 2 * cps, 2 * cps), :] = block
-        rows_turned[pl.ds(part * 2 * cps, 2 * cps), :] = turned(block)
-    returned = [solve(0, d, faces) for d in range(2)]
-
-    loads[4].wait()
-    for j in range(trace // 384):
-        whole = apply_map(j)
-        whole = whole[: 2 * cps] + whole[2 * cps :]
-        image[:, pl.ds(384 * j, 384)] = whole
-        image_out[:, pl.ds(384 * j, 384)] = whole.astype(BF16)
-    assemble(0, returned)
-
-    coming = gather_start(0, project(updated[0]))
-    moving = [gather_group(0, coming, *groups[0])]
-    image_coming = [
-        remote(image_out.at[:, pl.ds(d * pair, 256)], image_in.at[d], below[d]) for d in range(2)
-    ]
-    high = updated[0].astype(BF16)
-    rows[...] = high
-    rows_turned[...] = turned(high)
-    for j in range(trace // 384):
-        span = pl.ds(384 * j, 384)
-        outgoing[1, :, span] = (apply_map(j) + src[:, span]).astype(BF16)
-        if j + 1 < len(groups):
-            moving.append(gather_group(0, coming, *groups[j + 1]))
-    faces_next = send_faces(1)
 
     image_returned = []
     for d in range(2):
         image_coming[d].wait_recv()
-        upper = image_in[d].astype(F32)
-        own = image_out[:, pl.ds(d * pair, pair)].astype(F32)
+        head, tail = face_parts(image_in[d])
+        own = image[:, pl.ds(d * pair, pair)]
         low_lane = lanes(2 * cps) < 64
         zero = jnp.zeros((2 * cps, 128), F32)
         x = jnp.concatenate(
             [zero, jnp.where(low_lane, 0.0, own[:, 128:256]), own[:, 256:]], axis=1
         ).astype(BF16)
         w = jnp.concatenate(
-            [upper[:, :128], jnp.where(low_lane, upper[:, 128:], 0.0), zero], axis=1
+            [head, jnp.where(low_lane, tail, 0.0), zero], axis=1
         ).astype(BF16)
         solved = dot(jnp.concatenate([x, w], axis=0), solver[d, 0]) + dot(
             jnp.concatenate([turned(x), turned(w)], axis=0), solver[d, 1]
         )
-        ret_out[2, d] = solved[:, :256].astype(BF16)
+        ret_out[2, d] = packed_face(solved)
         image_solved[d] = solved[:, 128:]
         image_returned.append(remote(ret_out.at[2, d], ret_in.at[2, d], above[d]))
-    first_squares = source_sums(updated[0] * updated[0])
     gram = dot_nt(both[:cps], both[:cps], HIGHEST) + dot_nt(both[cps:], both[cps:], HIGHEST)
     for c in range(2):
         basis_k[c] = three(both[c * cps : (c + 1) * cps])
-    split_at = groups[-1][0]
-    coming = gather_core(0, sum(moving[:-1], []), 0, split_at)
-    returned = [solve(1, d, faces_next) for d in range(2)]
-    coming += gather_core(0, moving[-1], split_at, nz)
-
-    inverse_coming.wait_recv()
-    coarse = coarse_of(0, coming)
-    high, low = split(coarse)
-    near_out[...] = jnp.where(
-        lanes(cps) < 64, high.astype(F32), pltpu.roll(low.astype(F32), sources, 1)
-    ).astype(BF16)
-    near_coming = []
-    for d in range(2):
-        near_coming.append(remote(near_out, near_in.at[2 * d], above[d]))
-        near_coming.append(remote(near_out, near_in.at[2 * d + 1], below[d]))
-    first_row = jnp.where(lanes(8) < 64, first_squares, energy_of(coarse))
-
-    assemble(1, returned)
-    state[...] = updated[1] - updated[0]
-    early = gather_start(2, project(state[...]))
+    assemble(0, returned)
+
+    coming = gather_start(0, project(updated[0]))
+    inverse_coming = remote(inv_all.at[:, :, col], inv_all.at[:, :, col], col_peer)
+    moving = [gather_group(0, coming, *groups[0])]
+    high = updated[0].astype(BF16)
+    rows[...] = high
+    rows_turned[...] = turned(high)
+    faces_next = []
+    for j in range(trace // 384):
+        span = pl.ds(384 * j, 384)
+        outgoing[1, :, span] = (apply_map(j) + src[:, span]).astype(BF16)
+        if j < 2:
+            faces_next.append(send_face(1, j))
+        if j + 1 < len(groups):
+            moving.append(gather_group(0, coming, *groups[j + 1]))
+
+    first_squares = source_sums(updated[0] * updated[0])
     for d in range(2):
         image_returned[d].wait_recv()
-        back = jnp.where(position[d] > 0, ret_in[2, d].astype(F32), 0.0)
+        back = jnp.concatenate(face_parts(ret_in[2, d]), axis=1)
+        back = jnp.where(position[d] > 0, back, 0.0)
         own = jnp.where(position[d] < last[d], image_solved[d], 0.0)
         for target, r, o in ((mapped, 2 * cps, 0), (mapped_near, 0, 2 * cps)):
             target[:, pl.ds(d * pair, 128)] = back[r : r + 2 * cps, :128]
@@ -421,6 +419,27 @@
     for c in range(2):
         mapped_end[c] = three(mapped[pl.ds(c * cps, cps), pl.ds(2 * pair, pair)])
     kernel_t[...] = jnp.concatenate(blocks, axis=0).T
+
+    split_at = groups[-1][0]
+    coming = gather_core(0, sum(moving[:-1], []), 0, split_at)
+    coming += gather_core(0, moving[-1], split_at, nz)
+    returned = [solve(1, d, faces_next) for d in range(2)]
+
+    inverse_coming.wait_recv()
+    coarse = coarse_of(0, coming)
+    high, low = split(coarse)
+    near_out[...] = jnp.where(
+        lanes(cps) < 64, high.astype(F32), pltpu.roll(low.astype(F32), sources, 1)
+    ).astype(BF16)
+    near_coming = []
+    for d in range(2):
+        near_coming.append(remote(near_out, near_in.at[2 * d], above[d]))
+        near_coming.append(remote(near_out, near_in.at[2 * d + 1], below[d]))
+    first_row = jnp.where(lanes(8) < 64, first_squares, energy_of(coarse))
+
+    assemble(1, returned)
+    state[...] = updated[1] - updated[0]
+    early = gather_start(2, project(state[...]))
 
     arrive(near_coming)
     near = [coarse]
@@ -480,6 +499,9 @@
     nm = nh * ny
     copies = 1 + 3 * 4 + 4 + 3 * (nz - 1) + 9 * (nm - 1) + 5 * (nc - 1)
     copies += 2 * (nz - 1 + nm * nc - 1)
+    def keep(array):
+        return pltpu.with_memory_space_constraint(array, pltpu.HBM)
+
     hbm = pl.BlockSpec(memory_space=pltpu.HBM)
     out = pl.pallas_call(
         functools.partial(kernel, shape),
@@ -495,11 +517,12 @@
             pltpu.VMEM((2, 2, pair, pair), BF16),
             pltpu.VMEM((nz, 2, ncol, cps // 2, nm * nc * cps // 2), BF16),
             pltpu.VMEM((2, 2 * here, trace), BF16),
-            pltpu.VMEM((2 * cps, trace), BF16),
-            pltpu.VMEM((2, 2, 2 * here, 256), BF16),
-            pltpu.VMEM((2, 2 * cps, 256), BF16),
-            pltpu.VMEM((3, 2, 2 * here, 256), BF16),
-            pltpu.VMEM((3, 2, 2 * here, 256), BF16),
+            pltpu.VMEM((2, 3 * cps, 128), BF16),
+            pltpu.VMEM((2, 2, 3 * here, 128), BF16),
+            pltpu.VMEM((2, 2, 3 * here, 128), BF16),
+            pltpu.VMEM((2, 3 * cps, 128), BF16),
+            pltpu.VMEM((3, 2, 3 * here, 128), BF16),
+            pltpu.VMEM((3, 2, 3 * here, 128), BF16),
             pltpu.VMEM((2, 2 * here, 256), F32),
             pltpu.VMEM((2, 2 * here, trace), F32),
             pltpu.VMEM((2 * here, trace), F32),
@@ -518,22 +541,22 @@
             pltpu.VMEM((cps, 128), BF16),
             pltpu.VMEM((4, cps, 128), BF16),
             pltpu.VMEM((3, nz, nm, nc, cps // 2, 128), BF16),
-            pltpu.VMEM((2, nz, 8, 128), F32),
-            pltpu.VMEM((2, nm * nc, 8, 128), F32),
+            pltpu.VMEM((2, nz, 1, 128), F32),
+            pltpu.VMEM((2, nm * nc, 1, 128), F32),
             pltpu.SemaphoreType.DMA((5,)),
             pltpu.SemaphoreType.DMA((copies,)),
             pltpu.SemaphoreType.DMA((copies,)),
         ],
         compiler_params=pltpu.CompilerParams(
-            collective_id=0, has_side_effects=True, vmem_limit_bytes=60 * 1024 * 1024
+            collective_id=0, has_side_effects=True, vmem_limit_bytes=50 * 1024 * 1024
         ),
     )(
         lead_side.reshape(2),
-        sources.reshape(2 * here, trace),
-        impedance.reshape(2 * trace, trace),
-        pair_maps.reshape(4, pair, pair),
-        coarse_basis[0, 0],
-        coarse_inverse,
+        keep(sources.reshape(2 * here, trace)),
+        keep(impedance.reshape(2 * trace, trace)),
+        keep(pair_maps.reshape(4, pair, pair)),
+        keep(coarse_basis[0, 0]),
+        keep(coarse_inverse),
     )
     return out.reshape(1, 1, 2, here, trace)
 

time: 69.1 us -> 65.4 us (0.946)
  Pallas kernels: 67 us -> 63.8 us
    pallas_call x1, Pallas kernels: 67 us -> 63.8 us  [per_device(): pl.pallas_call(functools.partial(kernel, shape), out_shape=jax.ShapeDtype...]
    unnamed x1 -> x3, local copies, waits for them, and re-layouts: 1.92 us -> 1.47 us
where the time goes in v4:
time: 65.4 us; the launch traced here: 65.3 us
  Pallas kernels  63.8 us (98%)
  local copies, waits for them, and re-layouts  1.47 us (2%)
    pallas_call x1, Pallas kernels, per_device(): pl.pallas_call(functools.partial(kernel, shape), out_shape=jax.ShapeDtype...  63.8 us
    unnamed x3, local copies, waits for them, and re-layouts  1.47 us

profile of v4, /device:TPU:1, one launch (start us, length us, event | category | flops | bytes accessed | tf_op | source)
XLA Modules:
  0.0 65.3 jit_solution(621613426974258001)
XLA Ops:
  0.0 0.0 copy-start
  0.0 0.7 %copy-done = s32[1,1,2]{2,1,0:T(1,128)S(1)} copy-done((s32[1,1,2]{2,1,0:T(1,128)S(1)}, s32[1,1,2]{2,1,0:T(1,128)}, u32[]{:S(2)}) %copy-start) | copy-done | bytes 32
  0.7 63.8 %shard_map.64 = f32[128,1152]{1,0:T(8,128)S(1)} custom-call(s32[2]{0:T(128)S(1)} %bitcast.7, f32[128,1152]{1,0:T(8,128)} %bitcast.10, bf16[2304,1152]{1,0:T(8,128)(2,1)} %bitcast.8, bf16[4,384,384]{2,1,0:T(8,128)(2,1)} %bitcast.9, f32[32,2,1152]{2,1,0:T(2,128)} %bitcast.11, f32[16,4096]{1,0:T(8,128)} %inv_hbm.1), custom_call_target="tpu_custom_call" | custom-call | tf_op jit(solution)/shard_map/pallas_call | solution.py:506
  64.5 0.8 %copy.8 = f32[1,1,2,64,1152]{4,3,2,1,0:T(8,128)} copy(f32[1,1,2,64,1152]{4,3,2,1,0:T(8,128)S(1)} %bitcast.6) | data formatting | bytes 1179648
Async XLA Ops:
  0.0 0.7 %copy-start = (s32[1,1,2]{2,1,0:T(1,128)S(1)}, s32[1,1,2]{2,1,0:T(1,128)}, u32[]{:S(2)}) copy-start(s32[1,1,2]{2,1,0:T(1,128)} %param.9) | copy-start | bytes 28

commit v5 on v4

--- a/solution.py
+++ b/solution.py
@@ -238,9 +238,9 @@
     def gather_start(it, block):
         gathered[it, 0, m, core] = block
         own = gathered.at[it, 0, m, core]
-        coming = [None]
-        for i in range(1, nz):
-            coming.append(remote(own, gathered.at[it, i, m, core], z_peers[offsets[i] - 1]))
+        coming = [None] * nz
+        for i in range(nz - 1, 0, -1):
+            coming[i] = remote(own, gathered.at[it, i, m, core], z_peers[offsets[i] - 1])
         return coming
 
     def gather_group(it, coming, low, high):
@@ -296,6 +296,20 @@
         )
         return dot_tn(coefficients, mapped_k[c, d])
 
+    def against_basis(block, c, start, width):
+        high, low = split(block)
+        first = dot_nt(
+            jnp.concatenate([high, low], axis=0),
+            proj_rows[pl.ds(c * cps, cps), pl.ds(start, width)],
+        )
+        second = dot_nt(high, proj_rows[pl.ds((2 + c) * cps, cps), pl.ds(start, width)])
+        return first[: block.shape[0]] + first[block.shape[0] :] + second
+
+    def sides_of(c, d):
+        part = mapped_near[pl.ds(c * cps, cps), pl.ds(d * pair, pair)]
+        left = lax.broadcasted_iota(jnp.int32, (cps, pair), 1) < face
+        return jnp.concatenate([jnp.where(left, part, 0.0), jnp.where(left, 0.0, part)], axis=0)
+
     loads[0].wait()
     outgoing[0] = src[...].astype(BF16)
     pl.semaphore_wait(barrier, len(partners))
@@ -319,9 +333,12 @@
         return whole
 
     image_coming = []
-    for j in range(2):
+
+    def send_image(j):
         image_out[j] = packed_face(apply_to_basis(j))
         image_coming.append(remote(image_out.at[j], image_in.at[j], below[j]))
+
+    send_image(0)
     loads[1].wait()
     for d in range(2):
         for c in range(2):
@@ -329,7 +346,9 @@
             swapped = jnp.concatenate([stored[face:], stored[:face]], axis=0)
             swapped = pltpu.roll(swapped, face, 1)
             solver[d, c] = jnp.where(lead_ref[d] == 0, swapped, stored).astype(BF16)
-    returned = [solve(0, d, faces) for d in range(2)]
+    returned = [solve(0, 0, faces)]
+    send_image(1)
+    returned.append(solve(0, 1, faces))
     apply_to_basis(2)
 
     loads[3].wait()
@@ -378,14 +397,33 @@
     rows_turned[...] = turned(high)
     faces_next = []
     for j in range(trace // 384):
+        if j == 2:
+            for group in groups[3:]:
+                moving.append(gather_group(0, coming, *group))
         span = pl.ds(384 * j, 384)
         outgoing[1, :, span] = (apply_map(j) + src[:, span]).astype(BF16)
         if j < 2:
             faces_next.append(send_face(1, j))
-        if j + 1 < len(groups):
-            moving.append(gather_group(0, coming, *groups[j + 1]))
+            if j + 1 < len(groups):
+                moving.append(gather_group(0, coming, *groups[j + 1]))
 
     first_squares = source_sums(updated[0] * updated[0])
+    split_at = groups[-1][0]
+    returned = [solve(1, d, faces_next) for d in range(2)]
+    coming = gather_core(0, sum(moving[:-1], []), 0, split_at)
+    coming += gather_core(0, moving[-1], split_at, nz)
+
+    inverse_coming.wait_recv()
+    coarse = coarse_of(0, coming)
+    high, low = split(coarse)
+    near_out[...] = jnp.where(
+        lanes(cps) < 64, high.astype(F32), pltpu.roll(low.astype(F32), sources, 1)
+    ).astype(BF16)
+    near_coming = []
+    for d in range(2):
+        near_coming.append(remote(near_out, near_in.at[2 * d], above[d]))
+        near_coming.append(remote(near_out, near_in.at[2 * d + 1], below[d]))
+    first_row = jnp.where(lanes(8) < 64, first_squares, energy_of(coarse))
     for d in range(2):
         image_returned[d].wait_recv()
         back = jnp.concatenate(face_parts(ret_in[2, d]), axis=1)
@@ -400,42 +438,15 @@
     mapped[:, pl.ds(2 * pair, pair)] = pltpu.roll(image[:, pl.ds(2 * pair, pair)], face, 1)
     moved = mapped[...] - both
     blocks = [
-        dot_nt(moved[:cps], both[:cps], HIGHEST) + dot_nt(moved[cps:], both[cps:], HIGHEST)
+        against_basis(moved[:cps], 0, 0, trace) + against_basis(moved[cps:], 1, 0, trace)
     ]
-    left = lax.broadcasted_iota(jnp.int32, (cps, pair), 1) < face
     for d in range(2):
-        total = 0.0
-        for c in range(2):
-            part = mapped_near[pl.ds(c * cps, cps), pl.ds(d * pair, pair)]
-            sides = jnp.concatenate([jnp.where(left, part, 0.0), jnp.where(left, 0.0, part)], axis=0)
-            total = total + dot_nt(
-                sides, both[c * cps : (c + 1) * cps, d * pair : (d + 1) * pair], HIGHEST
-            )
-            own = three(mapped[pl.ds(c * cps, cps), pl.ds(d * pair, pair)])
-            mapped_k[c, d] = jnp.concatenate(
-                [own, three(sides[:cps]), three(sides[cps:])], axis=0
-            )
-        blocks.append(total)
-    for c in range(2):
-        mapped_end[c] = three(mapped[pl.ds(c * cps, cps), pl.ds(2 * pair, pair)])
+        blocks.append(
+            against_basis(sides_of(0, d), 0, d * pair, pair)
+            + against_basis(sides_of(1, d), 1, d * pair, pair)
+        )
     kernel_t[...] = jnp.concatenate(blocks, axis=0).T
 
-    split_at = groups[-1][0]
-    coming = gather_core(0, sum(moving[:-1], []), 0, split_at)
-    coming += gather_core(0, moving[-1], split_at, nz)
-    returned = [solve(1, d, faces_next) for d in range(2)]
-
-    inverse_coming.wait_recv()
-    coarse = coarse_of(0, coming)
-    high, low = split(coarse)
-    near_out[...] = jnp.where(
-        lanes(cps) < 64, high.astype(F32), pltpu.roll(low.astype(F32), sources, 1)
-    ).astype(BF16)
-    near_coming = []
-    for d in range(2):
-        near_coming.append(remote(near_out, near_in.at[2 * d], above[d]))
-        near_coming.append(remote(near_out, near_in.at[2 * d + 1], below[d]))
-    first_row = jnp.where(lanes(8) < 64, first_squares, energy_of(coarse))
 
     assemble(1, returned)
     state[...] = updated[1] - updated[0]
@@ -451,6 +462,14 @@
     )
     norms = share(sum_z, 0, z, z_peers, first_row)
     moving = [gather_group(1, coming, *groups[0])]
+    for c in range(2):
+        for d in range(2):
+            sides = sides_of(c, d)
+            own = three(mapped[pl.ds(c * cps, cps), pl.ds(d * pair, pair)])
+            mapped_k[c, d] = jnp.concatenate(
+                [own, three(sides[:cps]), three(sides[cps:])], axis=0
+            )
+        mapped_end[c] = three(mapped[pl.ds(c * cps, cps), pl.ds(2 * pair, pair)])
     early = gather_group(2, early, 0, nz)
     for c in range(2):
         part = pl.ds(c * sources, sources)

time: 65.4 us -> 62.4 us (0.954)
  Pallas kernels: 63.8 us -> 60.8 us
    pallas_call x1, Pallas kernels: 63.8 us -> 60.8 us  [per_device(): pl.pallas_call(functools.partial(kernel, shape), out_shape=jax.ShapeDtype...]
where the time goes in v5:
time: 62.4 us; the launch traced here: 62.3 us
  Pallas kernels  60.8 us (97%)
  local copies, waits for them, and re-layouts  1.47 us (2%)
    pallas_call x1, Pallas kernels, per_device(): pl.pallas_call(functools.partial(kernel, shape), out_shape=jax.ShapeDtype...  60.8 us
    unnamed x3, local copies, waits for them, and re-layouts  1.47 us

profile of v5, /device:TPU:1, one launch (start us, length us, event | category | flops | bytes accessed | tf_op | source)
XLA Modules:
  0.0 62.3 jit_solution(8177206087693981282)
XLA Ops:
  0.0 0.0 copy-start
  0.0 0.7 %copy-done = s32[1,1,2]{2,1,0:T(1,128)S(1)} copy-done((s32[1,1,2]{2,1,0:T(1,128)S(1)}, s32[1,1,2]{2,1,0:T(1,128)}, u32[]{:S(2)}) %copy-start) | copy-done | bytes 32
  0.7 60.8 %shard_map.64 = f32[128,1152]{1,0:T(8,128)S(1)} custom-call(s32[2]{0:T(128)S(1)} %bitcast.7, f32[128,1152]{1,0:T(8,128)} %bitcast.10, bf16[2304,1152]{1,0:T(8,128)(2,1)} %bitcast.8, bf16[4,384,384]{2,1,0:T(8,128)(2,1)} %bitcast.9, f32[32,2,1152]{2,1,0:T(2,128)} %bitcast.11, f32[16,4096]{1,0:T(8,128)} %inv_hbm.1), custom_call_target="tpu_custom_call" | custom-call | tf_op jit(solution)/shard_map/pallas_call | solution.py:525
  61.5 0.8 %copy.8 = f32[1,1,2,64,1152]{4,3,2,1,0:T(8,128)} copy(f32[1,1,2,64,1152]{4,3,2,1,0:T(8,128)S(1)} %bitcast.6) | data formatting | bytes 1179648
Async XLA Ops:
  0.0 0.7 %copy-start = (s32[1,1,2]{2,1,0:T(1,128)S(1)}, s32[1,1,2]{2,1,0:T(1,128)}, u32[]{:S(2)}) copy-start(s32[1,1,2]{2,1,0:T(1,128)} %param.9) | copy-start | bytes 28

commit v6 on v5

--- a/solution.py
+++ b/solution.py
@@ -384,9 +384,6 @@
         ret_out[2, d] = packed_face(solved)
         image_solved[d] = solved[:, 128:]
         image_returned.append(remote(ret_out.at[2, d], ret_in.at[2, d], above[d]))
-    gram = dot_nt(both[:cps], both[:cps], HIGHEST) + dot_nt(both[cps:], both[cps:], HIGHEST)
-    for c in range(2):
-        basis_k[c] = three(both[c * cps : (c + 1) * cps])
     assemble(0, returned)
 
     coming = gather_start(0, project(updated[0]))
@@ -408,6 +405,9 @@
                 moving.append(gather_group(0, coming, *groups[j + 1]))
 
     first_squares = source_sums(updated[0] * updated[0])
+    gram = dot_nt(both[:cps], both[:cps], HIGHEST) + dot_nt(both[cps:], both[cps:], HIGHEST)
+    for c in range(2):
+        basis_k[c] = three(both[c * cps : (c + 1) * cps])
     split_at = groups[-1][0]
     returned = [solve(1, d, faces_next) for d in range(2)]
     coming = gather_core(0, sum(moving[:-1], []), 0, split_at)

time: 62.4 us -> 62.3 us (level)
  no operation moved by 1% of the time
where the time goes in v6:
time: 62.3 us; the launch traced here: 62.2 us
  Pallas kernels  60.7 us (97%)
  local copies, waits for them, and re-layouts  1.47 us (2%)
    pallas_call x1, Pallas kernels, per_device(): pl.pallas_call(functools.partial(kernel, shape), out_shape=jax.ShapeDtype...  60.7 us
    unnamed x3, local copies, waits for them, and re-layouts  1.47 us

profile of v6, /device:TPU:1, one launch (start us, length us, event | category | flops | bytes accessed | tf_op | source)
XLA Modules:
  0.0 62.2 jit_solution(15894793442605810297)
XLA Ops:
  0.0 0.0 copy-start
  0.0 0.7 %copy-done = s32[1,1,2]{2,1,0:T(1,128)S(1)} copy-done((s32[1,1,2]{2,1,0:T(1,128)S(1)}, s32[1,1,2]{2,1,0:T(1,128)}, u32[]{:S(2)}) %copy-start) | copy-done | bytes 32
  0.7 60.7 %shard_map.64 = f32[128,1152]{1,0:T(8,128)S(1)} custom-call(s32[2]{0:T(128)S(1)} %bitcast.7, f32[128,1152]{1,0:T(8,128)} %bitcast.10, bf16[2304,1152]{1,0:T(8,128)(2,1)} %bitcast.8, bf16[4,384,384]{2,1,0:T(8,128)(2,1)} %bitcast.9, f32[32,2,1152]{2,1,0:T(2,128)} %bitcast.11, f32[16,4096]{1,0:T(8,128)} %inv_hbm.1), custom_call_target="tpu_custom_call" | custom-call | tf_op jit(solution)/shard_map/pallas_call | solution.py:525
  61.4 0.8 %copy.8 = f32[1,1,2,64,1152]{4,3,2,1,0:T(8,128)} copy(f32[1,1,2,64,1152]{4,3,2,1,0:T(8,128)S(1)} %bitcast.6) | data formatting | bytes 1179648
Async XLA Ops:
  0.0 0.7 %copy-start = (s32[1,1,2]{2,1,0:T(1,128)S(1)}, s32[1,1,2]{2,1,0:T(1,128)}, u32[]{:S(2)}) copy-start(s32[1,1,2]{2,1,0:T(1,128)} %param.9) | copy-start | bytes 28

commit v7 on v6

--- a/solution.py
+++ b/solution.py
@@ -31,6 +31,13 @@
 def split(x):
     high = x.astype(BF16)
     return high, (x - high.astype(F32)).astype(BF16)
+
+
+def dot_three(a, b):
+    high, low = split(a)
+    b_high, b_low = split(b)
+    first = dot(jnp.concatenate([high, low], axis=0), b_high)
+    return first[: a.shape[0]] + first[a.shape[0] :] + dot(high, b_low)
 
 
 def kernel(
@@ -281,7 +288,7 @@
         return STEP_RATIO * jnp.sqrt(total / (pltpu.roll(total, sources, 1) + 1e-06))
 
     def energy_of(coarse):
-        energy = jnp.sum(coarse * dot(gram, coarse, HIGHEST), axis=0, keepdims=True)
+        energy = jnp.sum(coarse * dot_three(gram, coarse), axis=0, keepdims=True)
         return pltpu.roll(jnp.broadcast_to(energy, (8, 128)), sources, 1)
 
     def three(block):
@@ -458,7 +465,7 @@
         both_parts = near_in[i].astype(F32)
         near.append(both_parts + pltpu.roll(both_parts, sources, 1))
     coming = gather_start(
-        1, packed(dot(kernel_t[...], jnp.concatenate(near, axis=0), HIGHEST))
+        1, packed(dot_three(kernel_t[...], jnp.concatenate(near, axis=0)))
     )
     norms = share(sum_z, 0, z, z_peers, first_row)
     moving = [gather_group(1, coming, *groups[0])]
@@ -494,12 +501,16 @@
     row = jnp.where(lanes(8) < 64, squares, energy_of(coarse))
     norms = share(sum_z, 1, z, z_peers, row)
     near = [factor[0:1] * part for part in near]
-    for c in range(2):
+
+    def finish_update(c):
         part = pl.ds(c * sources, sources)
         for d in range(3):
             span = pl.ds(d * pair, pair)
             updated[1, part, span] = updated[1, part, span] + mapped_sum(near, c, d)
+
+    finish_update(0)
     norms = share(sum_q, 1, q, q_peers, added(sum_z, 1, norms))
+    finish_update(1)
     factor = factor_of(added(sum_q, 1, norms))
     scaled = stacked(factor[0:1] * coarse)
     for c in range(2):

time: 62.3 us -> 62.3 us (level)
  no operation moved by 1% of the time
where the time goes in v7:
time: 62.3 us; the launch traced here: 62.2 us
  Pallas kernels  60.7 us (97%)
  local copies, waits for them, and re-layouts  1.47 us (2%)
    pallas_call x1, Pallas kernels, per_device(): pl.pallas_call(functools.partial(kernel, shape), out_shape=jax.ShapeDtype...  60.7 us
    unnamed x3, local copies, waits for them, and re-layouts  1.47 us

profile of v7, /device:TPU:1, one launch (start us, length us, event | category | flops | bytes accessed | tf_op | source)
XLA Modules:
  0.0 62.2 jit_solution(15007944793320044286)
XLA Ops:
  0.0 0.0 copy-start
  0.0 0.7 %copy-done = s32[1,1,2]{2,1,0:T(1,128)S(1)} copy-done((s32[1,1,2]{2,1,0:T(1,128)S(1)}, s32[1,1,2]{2,1,0:T(1,128)}, u32[]{:S(2)}) %copy-start) | copy-done | bytes 32
  0.7 60.7 %shard_map.64 = f32[128,1152]{1,0:T(8,128)S(1)} custom-call(s32[2]{0:T(128)S(1)} %bitcast.7, f32[128,1152]{1,0:T(8,128)} %bitcast.10, bf16[2304,1152]{1,0:T(8,128)(2,1)} %bitcast.8, bf16[4,384,384]{2,1,0:T(8,128)(2,1)} %bitcast.9, f32[32,2,1152]{2,1,0:T(2,128)} %bitcast.11, f32[16,4096]{1,0:T(8,128)} %inv_hbm.1), custom_call_target="tpu_custom_call" | custom-call | tf_op jit(solution)/shard_map/pallas_call | solution.py:536
  61.4 0.8 %copy.8 = f32[1,1,2,64,1152]{4,3,2,1,0:T(8,128)} copy(f32[1,1,2,64,1152]{4,3,2,1,0:T(8,128)S(1)} %bitcast.6) | data formatting | bytes 1179648
Async XLA Ops:
  0.0 0.7 %copy-start = (s32[1,1,2]{2,1,0:T(1,128)S(1)}, s32[1,1,2]{2,1,0:T(1,128)}, u32[]{:S(2)}) copy-start(s32[1,1,2]{2,1,0:T(1,128)} %param.9) | copy-start | bytes 28
